TPU v7x, 8 devices: a whole 2x2x1 slice. The times are simulated.
8 devices in a mesh: dp: 2 (over z, y), tp: 4 (over x, core).
Axes of the slice: x: 2, y: 2, z: 1, core: 2. Of those that a mesh axis runs over, the one named last changes fastest.
Arguments:
- x: bfloat16 [32, 1536], P('dp'), parts along dimension 0
- k_cache: bfloat16 [32, 4096, 12, 128], P('dp', None, 'tp'), parts along dimension 0
- v_cache: bfloat16 [32, 4096, 12, 128], P('dp', None, 'tp'), parts along dimension 0
- seq_lens: int32 [32], P('dp'), parts along dimension 0
- nbr_enc: bfloat16 [32, 256, 896], P('dp', 'tp'), parts along dimension 0
- ln1_gain: float32 [1536], replicated
- ln1_bias: float32 [1536], replicated
- w_q: bfloat16 [1536, 1536], P(None, 'tp')
- w_k: bfloat16 [1536, 1536], P(None, 'tp')
- w_v: bfloat16 [1536, 1536], P(None, 'tp')
- w_o: bfloat16 [1536, 1536], P('tp')
- ln2_gain: float32 [1536], replicated
- ln2_bias: float32 [1536], replicated
- wq_c: bfloat16 [1536, 1536], P(None, 'tp')
- wk_c: bfloat16 [896, 1536], P(None, 'tp')
- wv_c: bfloat16 [896, 1536], P(None, 'tp')
- wo_c: bfloat16 [1536, 1536], P('tp')
- ln3_gain: float32 [1536], replicated
- ln3_bias: float32 [1536], replicated
- w_up: bfloat16 [1536, 6144], P(None, 'tp')
- w_down: bfloat16 [6144, 1536], P('tp')
Outputs:
- output 1: bfloat16 [32, 1536], P('dp'), parts along dimension 0
- output 2: bfloat16 [32, 12, 128], P('dp', 'tp'), parts along dimension 0
- output 3: bfloat16 [32, 12, 128], P('dp', 'tp'), parts along dimension 0
There are 2 independent parts. A program takes and returns all parts, laid end to end along the dimension named above; an argument that names none is the same for every part.
All inputs are finite; a program needn't handle non-finite values.
Results may differ from a plain program's by a relative error of at most 0.0147339.
Values are sent between devices in bfloat16 or wider.
A program may use at most 1 GiB of HBM per device.

v0:
```python
import functools

import jax
import jax.numpy as jnp
from jax import lax
from jax.experimental import pallas as pl
from jax.experimental.pallas import tpu as pltpu
from jax.sharding import PartitionSpec as P


LN_EPS = 1e-5
NEG = -1e30
F32 = jnp.float32
BF16 = jnp.bfloat16
CHUNK = 512
UNROLL = 4
GRAIN = 64
GROUPS = 6


def layer_norm(values, ln_gain, ln_bias):
    row_mean = jnp.mean(values, axis=-1, keepdims=True)
    centred = values - row_mean
    row_var = jnp.mean(jnp.square(centred), axis=-1, keepdims=True)
    return (centred * lax.rsqrt(row_var + LN_EPS) * ln_gain + ln_bias).astype(BF16)


def dot(lhs, rhs):
    return jnp.dot(lhs, rhs, preferred_element_type=F32)


def dot_t(lhs, rhs):
    return lax.dot_general(lhs, rhs, (((1,), (1,)), ((), ())), preferred_element_type=F32)


def in_hbm(*arrays):
    return [pltpu.with_memory_space_constraint(a, pltpu.HBM) for a in arrays]


def self_kernel(batch, heads, dim, lens_h, x_h, g_h, b_h, kc, vc, wq_h, wk_h, wv_h, wo_h,
                part_ref, knew_ref, vnew_ref,
                lens, x_v, g_v, b_v, wq, wk, wv, wo, kbuf, vbuf, q_s, v_s, o_s, m_s, l_s, acc_s, new_s, wsem, ksem, vsem):
    width = heads * dim
    scale = dim ** -0.5
    pairs = ((x_h, x_v), (g_h, g_v), (b_h, b_v), (wq_h, wq), (lens_h, lens), (wk_h, wk), (wv_h, wv), (wo_h, wo))
    ld_x, ld_g, ld_b, ld_q, ld_len, ld_k, ld_v, ld_o = [pltpu.make_async_copy(src, dst, wsem.at[i]) for i, (src, dst) in enumerate(pairs)]
    for copy in (ld_len, ld_x, ld_g, ld_b, ld_q, ld_k, ld_v):
        copy.start()

    def len_of(seq):
        return jnp.where(seq < batch, lens[jnp.minimum(seq, batch - 1)], 0)

    def following(seq, blk):
        more = (blk + 1) * CHUNK < len_of(seq)
        return jnp.where(more, seq, seq + 1), jnp.where(more, blk + 1, 0)

    def copies(seq, blk, slot, whole):
        live = pl.multiple_of(jnp.minimum(len_of(seq) - blk * CHUNK, CHUNK), GRAIN)
        first = pl.multiple_of(blk * CHUNK, CHUNK)
        count = CHUNK if whole else live
        src, dst = pl.ds(first, count), pl.ds(0, count)
        return (pltpu.make_async_copy(kc.at[seq, :, src, :], kbuf.at[slot, :, dst, :], ksem.at[slot]),
                pltpu.make_async_copy(vc.at[seq, :, src, :], vbuf.at[slot, :, dst, :], vsem.at[slot]))

    def fetch_group(group, ptr, whole):
        for u in range(UNROLL):
            seq, blk = ptr

            @pl.when(seq < batch)
            def _():
                for copy in copies(seq, blk, group * UNROLL + u, whole):
                    copy.start()

            ptr = following(seq, blk)
        return ptr

    ld_len.wait()
    ptr = (jnp.int32(0), jnp.int32(0))
    for group in range(GROUPS):
        ptr = fetch_group(group, ptr, True)
    ld_o.start()

    n_items = jnp.int32(0)
    for seq in range(batch):
        n_items = n_items + lax.div(lens[seq] + (CHUNK - 1), CHUNK)
    n_steps = lax.div(n_items + (UNROLL - 1), UNROLL)

    for copy in (ld_x, ld_g, ld_b):
        copy.wait()
    a_norm = layer_norm(x_v[...].astype(F32), g_v[...].reshape(1, -1), b_v[...].reshape(1, -1))
    ld_q.wait()
    q_s[0:batch, :] = dot(a_norm, wq[...]).astype(BF16).astype(F32)
    q_s[batch:, :] = jnp.zeros((q_s.shape[0] - batch, width), F32)
    m_s[...] = jnp.full(m_s.shape, NEG, F32)
    l_s[...] = jnp.zeros_like(l_s)
    acc_s[...] = jnp.zeros_like(acc_s)

    pair = 2 * dim
    part_rows = CHUNK // 2
    row8 = lax.broadcasted_iota(jnp.int32, (8, 1), 0)
    pair_row = lax.broadcasted_iota(jnp.int32, (8, pair), 0)
    pair_side = lax.broadcasted_iota(jnp.int32, (8, pair), 1) // dim
    sel01 = (pair_row == pair_side).astype(F32)
    sel2 = (pair_row == pair_side + 2).astype(F32)
    lane = lax.broadcasted_iota(jnp.int32, (8, CHUNK), 1)
    lane2 = lax.broadcasted_iota(jnp.int32, (8, part_rows), 1)

    def new_token():
        ld_k.wait()
        k_new = dot(a_norm, wk[...]).astype(BF16)
        ld_v.wait()
        v_new = dot(a_norm, wv[...]).astype(BF16)
        for h in range(heads):
            knew_ref[h] = k_new[:, h * dim:(h + 1) * dim]
            vnew_ref[h] = v_new[:, h * dim:(h + 1) * dim]
        qk = q_s[0:batch, :] * k_new.astype(F32)
        v_s[...] = v_new.astype(F32)
        for seq in range(batch):
            prod = qk[seq:seq + 1, :]
            tail = jnp.concatenate([prod[:, pair:width], jnp.zeros((1, pair - dim), F32)], axis=1)
            s_new = jnp.sum(prod[:, 0:pair] * sel01 + tail * sel2, axis=1, keepdims=True) * scale
            new_s[seq] = jnp.broadcast_to(jnp.where(row8 == 3, NEG, s_new), (8, dim))

    def step(i, carry):
        ptr, cur = carry[:2], carry[2:]
        group = lax.rem(i, GROUPS)

        @pl.when(i == 1)
        def _():
            new_token()

        items = []
        for u in range(UNROLL):
            items.append((*cur, group * UNROLL + u))
            cur = following(*cur)
        for seq, blk, slot in items:

            @pl.when((seq < batch) & (i < GROUPS))
            def _():
                for copy in copies(seq, blk, slot, True):
                    copy.wait()

            @pl.when((seq < batch) & (i >= GROUPS))
            def _():
                for copy in copies(seq, blk, slot, False):
                    copy.wait()
        scores = []
        for seq, blk, slot in items:
            q_row = q_s[pl.ds(jnp.minimum(seq, batch), 1), :]
            q01 = (q_row[:, 0:pair] * sel01).astype(BF16)
            q2 = (jnp.concatenate([q_row[:, pair:width]] * 2, axis=1) * sel2).astype(BF16)
            k01 = jnp.concatenate([kbuf[slot, 0], kbuf[slot, 1]], axis=1)
            k2 = jnp.concatenate([kbuf[slot, 2, 0:part_rows, :], kbuf[slot, 2, part_rows:CHUNK, :]], axis=1)
            scores.append((dot_t(q01, k01), dot_t(q2, k2)))
        weights = []
        for (seq, blk, slot), (s01, s2) in zip(items, scores):
            live = len_of(seq) - blk * CHUNK
            s01 = jnp.where(lane < jnp.where(row8 < 2, live, 0), s01 * scale, NEG)
            s2 = jnp.where(lane2 < jnp.where(row8 == 2, live, jnp.where(row8 == 3, live - part_rows, 0)), s2 * scale, NEG)
            m_i = jnp.maximum(jnp.max(s01, axis=1, keepdims=True), jnp.max(s2, axis=1, keepdims=True))
            p01 = jnp.where(row8 < 2, jnp.exp(s01 - m_i), 0.0)
            p2 = jnp.where(row8 < 2, 0.0, jnp.exp(s2 - m_i))
            l_i = jnp.sum(p01, axis=1, keepdims=True) + jnp.sum(p2, axis=1, keepdims=True)
            weights.append((m_i, l_i, p01.astype(BF16), p2.astype(BF16)))
        values = []
        for (seq, blk, slot), (m_i, l_i, p01, p2) in zip(items, weights):
            v01 = jnp.concatenate([vbuf[slot, 0], vbuf[slot, 1]], axis=1)
            v2 = jnp.concatenate([vbuf[slot, 2, 0:part_rows, :], vbuf[slot, 2, part_rows:CHUNK, :]], axis=1)
            values.append(dot(p01, v01) + dot(p2, v2))
        for (seq, blk, slot), (m_i, l_i, p01, p2), pv in zip(items, weights, values):
            row = jnp.minimum(seq, batch)
            m_old = m_s[row]
            m_new = jnp.maximum(m_old, m_i)
            keep = jnp.exp(m_old - m_new)
            add = jnp.exp(m_i - m_new)
            m_s[row] = m_new
            l_s[row] = l_s[row] * keep + l_i * add
            acc_s[row] = acc_s[row] * jnp.concatenate([keep] * 2, axis=1) + pv * jnp.concatenate([add] * 2, axis=1)
        ptr = fetch_group(group, ptr, False)
        return (*ptr, *cur)

    lax.fori_loop(0, n_steps, step, (*ptr, jnp.int32(0), jnp.int32(0)))
    for seq in range(batch):
        m_old, s_new = m_s[seq], new_s[seq]
        m = jnp.maximum(m_old, s_new)
        keep, add = jnp.exp(m_old - m), jnp.exp(s_new - m)
        v_row = v_s[seq:seq + 1, :]
        v_pair = jnp.where(pair_row < 2, v_row[:, 0:pair], jnp.concatenate([v_row[:, pair:width]] * 2, axis=1))
        l = l_s[seq] * keep + add
        acc = acc_s[seq] * jnp.concatenate([keep] * 2, axis=1) + v_pair * jnp.concatenate([add] * 2, axis=1)
        top = jnp.maximum(m[2:3], m[3:4])
        w_a, w_b = jnp.exp(m[2:3] - top), jnp.exp(m[3:4] - top)
        o2 = (acc[2:3, 0:dim] * w_a + acc[3:4, dim:pair] * w_b) / (l[2:3] * w_a + l[3:4] * w_b)
        o_s[seq:seq + 1, :] = jnp.concatenate([acc[0:1, 0:dim] / l[0:1], acc[1:2, dim:pair] / l[1:2], o2], axis=1)
    ld_o.wait()
    part_ref[...] = dot(o_s[...].astype(BF16), wo[...]).astype(BF16)


def rest_kernel(batch, heads, dim, tp, part_ref, x_ref, g2, b2, g3, b3, wqc_h, e_own_h, wk_h, wv_h, wkr_h, wvr_h, woc_h, wup_h, wdn_h,
                out_ref,
                wqc, enc, wkv, wkvr, woc, wup, wdn, kv_own, kv_rem, recv, send2, send3, qc_s, qc_r, o_snd, o_rcv,
                lsem, ssem, rsem, xs, xr, ns, nr):
    width = heads * dim
    scale = dim ** -0.5
    me = lax.axis_index('tp')
    far = lax.rem(me + 2, tp)
    near = me + 1 - 2 * lax.rem(me, 2)
    half = enc.shape[0] // 2
    early = wvr_h.shape[1]

    def load(i, src, dst):
        copy = pltpu.make_async_copy(src, dst, lsem.at[i])
        copy.start()
        return copy

    ld_e0 = load(0, e_own_h, enc.at[pl.ds(0, half), :])
    ld_wk = load(1, wk_h, wkv.at[:, pl.ds(0, width)])
    ld_wv = load(2, wv_h, wkv.at[:, pl.ds(width, width)])
    ld_wkr = load(3, wkr_h, wkvr.at[:, pl.ds(0, width)])
    ld_wvr = load(4, wvr_h, wkvr.at[:, pl.ds(width, early)])
    ld_wqc = load(5, wqc_h, wqc)
    ld_woc = load(6, woc_h, woc)
    ld_up = load(7, wup_h, wup)
    ld_dn = load(8, wdn_h, wdn)

    barrier = pltpu.get_barrier_semaphore()
    for d in range(1, tp):
        pl.semaphore_signal(barrier, inc=1, device_id={'tp': lax.rem(me + d, tp)}, device_id_type=pl.DeviceIdType.MESH)
    pl.semaphore_wait(barrier, tp - 1)

    def exchange(n, src):
        for d in range(1, tp):
            pltpu.make_async_remote_copy(src_ref=src, dst_ref=recv.at[n, me], send_sem=ssem.at[n, d - 1], recv_sem=rsem.at[n, me],
                                         device_id={'tp': lax.rem(me + d, tp)}, device_id_type=pl.DeviceIdType.MESH).start()
        recv[n, me] = src[...]

    def collect(n, src):
        for d in range(1, tp):
            other = lax.rem(me + d, tp)
            pltpu.make_async_remote_copy(src_ref=src, dst_ref=recv.at[n, other], send_sem=ssem.at[n, d - 1], recv_sem=rsem.at[n, other],
                                         device_id={'tp': other}, device_id_type=pl.DeviceIdType.MESH).wait()
        total = recv[n, 0].astype(F32)
        for t in range(1, tp):
            total = total + recv[n, t].astype(F32)
        return total

    def to_far(i, src, dst):
        return pltpu.make_async_remote_copy(src_ref=src, dst_ref=dst, send_sem=xs.at[i], recv_sem=xr.at[i],
                                            device_id={'tp': far}, device_id_type=pl.DeviceIdType.MESH)

    def project(first, count, jobs, tile=256):
        def body(i, c):
            rows = pl.ds(pl.multiple_of(i * tile, tile), tile)
            for weights, out, lo, hi in jobs:
                out[rows, lo:hi] = dot(enc[rows, :], weights[:, lo:hi]).astype(BF16)
            return c

        lax.fori_loop(first // tile, (first + count) // tile, body, 0)

    late_rows = (0, 640, wv_h.shape[0])

    def late(i):
        rows, cols = pl.ds(late_rows[i], late_rows[i + 1] - late_rows[i]), width - early
        return to_far(2 + i, wv_h.at[rows, pl.ds(early, cols)], wkvr.at[rows, pl.ds(width + early, cols)])

    exchange(0, part_ref)
    near_e = pltpu.make_async_remote_copy(src_ref=e_own_h, dst_ref=enc.at[pl.ds(half, half), :], send_sem=ns.at[0], recv_sem=nr.at[0],
                                          device_id={'tp': near}, device_id_type=pl.DeviceIdType.MESH)
    near_e.start()
    late(0).start()
    jobs = ((wkv, kv_own, 0, 2 * width), (wkvr, kv_rem, 0, width + early))
    for copy in (ld_e0, ld_wk, ld_wv, ld_wkr, ld_wvr):
        copy.wait()
    project(0, half, jobs)

    h1 = x_ref[...].astype(F32) + collect(0, part_ref)
    c_norm = layer_norm(h1, g2[...].reshape(1, -1), b2[...].reshape(1, -1))
    ld_wqc.wait()
    qc_s[...] = dot(c_norm, wqc[...]).astype(BF16)
    send_q = to_far(0, qc_s, qc_r)
    send_q.start()
    late(1).start()
    near_e.wait()
    project(half, half, jobs[1:])
    for i in range(2):
        late(i).wait()
    project(0, 2 * half, ((wkvr, kv_rem, width + early, 2 * width),))

    rows = heads * batch
    row_b = lax.rem(lax.broadcasted_iota(jnp.int32, (rows, 128), 0), batch)
    lane = lax.broadcasted_iota(jnp.int32, (rows, 128), 1)
    per = half // batch
    pack = 128 // per
    blocks = half // 128
    mine = lax.rem(row_b, pack) == lane // per
    row_blk = row_b // pack
    lane_head = lax.broadcasted_iota(jnp.int32, (batch, width), 1) // dim

    def attend(q, kv):
        qf = q.astype(F32)
        q_rows = jnp.concatenate([jnp.where(lane_head == h, qf, 0.0) for h in range(heads)], axis=0).astype(BF16)
        parts = []
        for part in range(2):
            s_all = dot_t(q_rows, kv[part * half:(part + 1) * half, 0:width])
            s = s_all[:, 0:128]
            for k in range(1, blocks):
                s = jnp.where(row_blk == k, s_all[:, k * 128:(k + 1) * 128], s)
            parts.append(jnp.where(mine, s * scale, NEG))
        m = jnp.maximum(jnp.max(parts[0], axis=1, keepdims=True), jnp.max(parts[1], axis=1, keepdims=True))
        p = [jnp.exp(s - m) for s in parts]
        l = jnp.sum(p[0], axis=1, keepdims=True) + jnp.sum(p[1], axis=1, keepdims=True)
        o = None
        for part in range(2):
            p_wide = jnp.concatenate([jnp.where(row_blk == k, p[part], 0.0) for k in range(blocks)], axis=1).astype(BF16)
            o_part = dot(p_wide, kv[part * half:(part + 1) * half, width:2 * width])
            o = o_part if o is None else o + o_part
        o = jnp.concatenate([o[h * batch:(h + 1) * batch, h * dim:(h + 1) * dim] for h in range(heads)], axis=0)
        return m, l, o

    send_q.wait()
    m_r, l_r, o_r = attend(qc_r[...], kv_rem)
    o_snd[0:rows, :] = o_r
    stats = jnp.zeros((batch, dim), F32)
    st_lane = lax.broadcasted_iota(jnp.int32, (batch, dim), 1)
    for h in range(heads):
        stats = jnp.where(st_lane == 2 * h, m_r[h * batch:(h + 1) * batch], jnp.where(st_lane == 2 * h + 1, l_r[h * batch:(h + 1) * batch], stats))
    o_snd[rows:rows + batch, :] = stats
    send_o = to_far(1, o_snd, o_rcv)
    send_o.start()
    project(half, half, jobs[:1])
    m_a, l_a, o_a = attend(qc_s[...], kv_own)
    send_o.wait()
    stats = o_rcv[rows:rows + batch, :]
    m_b = jnp.concatenate([stats[:, 2 * h:2 * h + 1] for h in range(heads)], axis=0)
    l_b = jnp.concatenate([stats[:, 2 * h + 1:2 * h + 2] for h in range(heads)], axis=0)
    m = jnp.maximum(m_a, m_b)
    w_a, w_b = jnp.exp(m_a - m), jnp.exp(m_b - m)
    o = (o_a * w_a + o_rcv[0:rows, :] * w_b) / (l_a * w_a + l_b * w_b)
    oc = jnp.concatenate([o[h * batch:(h + 1) * batch, :] for h in range(heads)], axis=1).astype(BF16)
    ld_woc.wait()
    send2[...] = dot(oc, woc[...]).astype(BF16)
    exchange(1, send2)
    h2 = h1 + collect(1, send2)
    m_norm = layer_norm(h2, g3[...].reshape(1, -1), b3[...].reshape(1, -1))
    ld_up.wait()
    up = dot(m_norm, wup[...])
    hidden = (0.5 * up * (1.0 + lax.erf(up * (0.5 ** 0.5)))).astype(BF16)
    ld_dn.wait()
    send3[...] = dot(hidden, wdn[...]).astype(BF16)
    exchange(2, send3)
    out_ref[...] = h2 + collect(2, send3)


def local_step(x, k_cache, v_cache, seq_lens, nbr_enc, ln1_gain, ln1_bias, w_q, w_k, w_v, w_o, ln2_gain, ln2_bias, wq_c, wk_c, wv_c, wo_c, ln3_gain, ln3_bias, w_up, w_down):
    batch, d_model = x.shape
    heads, dim = k_cache.shape[2:]
    width = heads * dim
    tp = lax.axis_size('tp')
    far = [(i, (i + 2) % tp) for i in range(tp)]
    enc = nbr_enc.reshape(-1, nbr_enc.shape[-1])
    wk_far = lax.ppermute(wk_c, 'tp', far)
    wv_cut = wv_c[:, :2 * dim]
    wv_far = lax.ppermute(wv_cut, 'tp', far)

    any_spec = pl.BlockSpec(memory_space=pl.ANY)
    hbm = pl.BlockSpec(memory_space=pltpu.HBM)
    vmem = pl.BlockSpec(memory_space=pltpu.VMEM)
    slots = GROUPS * UNROLL
    part, k_new, v_new = pl.pallas_call(
        functools.partial(self_kernel, batch, heads, dim),
        out_shape=(jax.ShapeDtypeStruct((batch, d_model), BF16), jax.ShapeDtypeStruct((heads, batch, dim), BF16), jax.ShapeDtypeStruct((heads, batch, dim), BF16)),
        in_specs=[hbm] * 10,
        out_specs=(vmem, vmem, vmem),
        scratch_shapes=[
            pltpu.SMEM((batch,), jnp.int32), pltpu.VMEM((batch, d_model), BF16), pltpu.VMEM((d_model,), F32), pltpu.VMEM((d_model,), F32),
            pltpu.VMEM((d_model, width), BF16), pltpu.VMEM((d_model, width), BF16), pltpu.VMEM((d_model, width), BF16), pltpu.VMEM((width, d_model), BF16),
            pltpu.VMEM((slots, heads, CHUNK, dim), BF16), pltpu.VMEM((slots, heads, CHUNK, dim), BF16),
            pltpu.VMEM((batch + 8, width), F32), pltpu.VMEM((batch, width), F32), pltpu.VMEM((batch, width), F32),
            pltpu.VMEM((batch + 1, 8, dim), F32), pltpu.VMEM((batch + 1, 8, dim), F32), pltpu.VMEM((batch + 1, 8, 2 * dim), F32), pltpu.VMEM((batch, 8, dim), F32),
            pltpu.SemaphoreType.DMA((8,)), pltpu.SemaphoreType.DMA((slots,)), pltpu.SemaphoreType.DMA((slots,)),
        ],
        compiler_params=pltpu.CompilerParams(vmem_limit_bytes=46000000),
        cost_estimate=pl.CostEstimate(flops=40_000_000_000, bytes_accessed=60_000_000, transcendentals=0),
        name='self_attention',
    )(*in_hbm(seq_lens, x, ln1_gain, ln1_bias, jnp.transpose(k_cache, (0, 2, 1, 3)), jnp.transpose(v_cache, (0, 2, 1, 3)), w_q, w_k, w_v, w_o))

    n_enc, enc_dim = enc.shape
    ff = w_up.shape[1]
    out = pl.pallas_call(
        functools.partial(rest_kernel, batch, heads, dim, tp),
        out_shape=jax.ShapeDtypeStruct((batch, d_model), F32),
        in_specs=[vmem] * 6 + [hbm] * 4 + [any_spec] * 2 + [hbm] * 3,
        out_specs=vmem,
        scratch_shapes=[
            pltpu.VMEM((d_model, width), BF16), pltpu.VMEM((2 * n_enc, enc_dim), BF16),
            pltpu.VMEM((enc_dim, 2 * width), BF16), pltpu.VMEM((enc_dim, 2 * width), BF16),
            pltpu.VMEM((width, d_model), BF16), pltpu.VMEM((d_model, ff), BF16), pltpu.VMEM((ff, d_model), BF16),
            pltpu.VMEM((2 * n_enc, 2 * width), BF16), pltpu.VMEM((2 * n_enc, 2 * width), BF16),
            pltpu.VMEM((3, tp, batch, d_model), BF16), pltpu.VMEM((batch, d_model), BF16), pltpu.VMEM((batch, d_model), BF16),
            pltpu.VMEM((batch, width), BF16), pltpu.VMEM((batch, width), BF16),
            pltpu.VMEM((heads * batch + batch, dim), F32), pltpu.VMEM((heads * batch + batch, dim), F32),
            pltpu.SemaphoreType.DMA((9,)), pltpu.SemaphoreType.DMA((3, tp - 1)), pltpu.SemaphoreType.DMA((3, tp)),
            pltpu.SemaphoreType.DMA((4,)), pltpu.SemaphoreType.DMA((4,)), pltpu.SemaphoreType.DMA((1,)), pltpu.SemaphoreType.DMA((1,)),
        ],
        compiler_params=pltpu.CompilerParams(collective_id=0, has_side_effects=True, vmem_limit_bytes=46000000),
        cost_estimate=pl.CostEstimate(flops=20_000_000_000, bytes_accessed=30_000_000, transcendentals=0),
        name='rest_of_layer',
    )(part, x, ln2_gain, ln2_bias, ln3_gain, ln3_bias, *in_hbm(wq_c, enc, wk_c, wv_c), wk_far, wv_far, *in_hbm(wo_c, w_up, w_down))
    return out.astype(BF16), jnp.transpose(k_new, (1, 0, 2)), jnp.transpose(v_new, (1, 0, 2))


def solution(mesh):
    row_spec = P('dp', None)
    cache_spec = P('dp', None, 'tp', None)
    head_spec = P('dp', 'tp', None)
    vec_spec = P(None)
    col_split = P(None, 'tp')
    row_split = P('tp', None)
    in_specs = (row_spec, cache_spec, cache_spec, P('dp'), P('dp', 'tp', None), vec_spec, vec_spec, col_split, col_split, col_split, row_split, vec_spec, vec_spec, col_split, col_split, col_split, row_split, vec_spec, vec_spec, col_split, row_split)
    out_specs = (row_spec, head_spec, head_spec)
    return jax.shard_map(local_step, mesh=mesh, in_specs=in_specs, out_specs=out_specs, check_vma=False)
```

profile of v0, /device:TPU:0, one launch (start us, length us, event | category | flops | bytes accessed | tf_op | source)
XLA Modules:
  0.0 57.6 jit_solution(12347448756390221280)
XLA Ops:
  0.6 1.1 %slice.3 = bf16[896,256]{1,0:T(8,128)(2,1)S(1)} slice(bf16[896,384]{1,0:T(8,128)(2,1)} %wv_h.3), slice={[0:896], [0:256]} | slice | bytes 917504 | tf_op jit(solution)/shard_map/slice | solution.py:362
  1.7 3.3 %collective-permute-start.1 = (bf16[896,256]{1,0:T(8,128)(2,1)S(1)}, bf16[896,256]{1,0:T(8,128)(2,1)S(1)}, u32[]{:S(2)}, u32[]{:S(2)}) collective-permute-start(bf16[896,256]{1,0:T(8,128)(2,1)S(1)} %slice.3), channel_id=1, source_target_pairs={{0,2},{1,3},{2,0},{3,1},{4,6},{5,7},{6,4},{7,5}} | collective-permute-start | bytes 1376264 | tf_op jit(solution)/shard_map/ppermute | solution.py:363
  5.0 0.0 collective-permute-start
  5.0 0.0 copy-start
  5.0 0.0 copy-start.1
  5.1 0.0 copy-start.2
  5.1 0.0 copy-start.3
  5.1 0.0 copy-start.4
  5.1 21.6 %self_attention.1 = (bf16[16,1536]{1,0:T(8,128)(2,1)S(1)}, bf16[3,16,128]{2,1,0:T(8,128)(2,1)}, bf16[3,16,128]{2,1,0:T(8,128)(2,1)}) custom-call(s32[16]{0:T(128)} %lens_h.1, bf16[16,1536]{1,0:T(8,128)(2,1)} %x_ref.1, f32[1536]{0:T(1024)} %g_h.1, f32[1536]{0:T(1024)} %b_h.1, bf16[16,3,4096,128]{3,2,1,0:T(8,128)(2,1)} %bitcast.5, ...), custom_call_target="tpu_custom_call" | custom-call | flops 40000000000 | bytes 60000000 | tf_op jit(solution)/shard_map/self_attention/pallas_call | solution.py:369
  26.7 0.0 collective-permute-done.1.wvr_h
  26.7 3.6 %collective-permute-done.wkr_h = bf16[896,384]{1,0:T(8,128)(2,1)S(1)} collective-permute-done((bf16[896,384]{1,0:T(8,128)(2,1)}, bf16[896,384]{1,0:T(8,128)(2,1)S(1)}, u32[]{:S(2)}, u32[]{:S(2)}) %collective-permute-start) | collective-permute-done | bytes 688160 | tf_op jit(solution)/shard_map/ppermute | solution.py:361
  30.3 0.0 copy-done
  30.3 0.0 copy-done.1
  30.3 0.0 copy-done.2
  30.3 0.0 copy-done.3
  30.3 0.0 copy-done.4
  30.3 26.7 %rest_of_layer.1 = f32[16,1536]{1,0:T(8,128)S(1)} custom-call(bf16[16,1536]{1,0:T(8,128)(2,1)S(1)} %get-tuple-element.6.part_ref, bf16[16,1536]{1,0:T(8,128)(2,1)S(1)} %copy-done, f32[1536]{0:T(1024)S(1)} %copy-done.1, f32[1536]{0:T(1024)S(1)} %copy-done.2, f32[1536]{0:T(1024)S(1)} %copy-done.3, f32[1536]{0:T(1024)S(1)} %copy-done.4, ...), custom_call_target="tpu_custom_call" | custom-call | flops 20000000000 | bytes 30000000 | tf_op jit(solution)/shard_map/rest_of_layer/pallas_call | solution.py:389
  57.0 0.6 %convert_element_type.3 = bf16[16,1536]{1,0:T(8,128)(2,1)} convert(f32[16,1536]{1,0:T(8,128)S(1)} %rest_of_layer.1) | non-fusion elementwise | flops 24576 | bytes 147456 | tf_op jit(solution)/shard_map/convert_element_type | solution.py:409
Async XLA Ops:
  1.7 25.0 %collective-permute-start.1 = (bf16[896,256]{1,0:T(8,128)(2,1)S(1)}, bf16[896,256]{1,0:T(8,128)(2,1)S(1)}, u32[]{:S(2)}, u32[]{:S(2)}) collective-permute-start(bf16[896,256]{1,0:T(8,128)(2,1)S(1)} %slice.3), channel_id=1, source_target_pairs={{0,2},{1,3},{2,0},{3,1},{4,6},{5,7},{6,4},{7,5}} | collective-permute-start | bytes 1376264 | tf_op jit(solution)/shard_map/ppermute | solution.py:363
  5.0 25.3 %collective-permute-start = (bf16[896,384]{1,0:T(8,128)(2,1)}, bf16[896,384]{1,0:T(8,128)(2,1)S(1)}, u32[]{:S(2)}, u32[]{:S(2)}) collective-permute-start(bf16[896,384]{1,0:T(8,128)(2,1)} %wk_h.3), channel_id=1, source_target_pairs={{0,2},{1,3},{2,0},{3,1},{4,6},{5,7},{6,4},{7,5}} | collective-permute-start | bytes 2064392 | tf_op jit(solution)/shard_map/ppermute | solution.py:361
  5.0 25.2 %copy-start = (bf16[16,1536]{1,0:T(8,128)(2,1)S(1)}, bf16[16,1536]{1,0:T(8,128)(2,1)}, u32[]{:S(2)}) copy-start(bf16[16,1536]{1,0:T(8,128)(2,1)} %x_ref.1) | copy-start | bytes 147460
  5.0 25.2 %copy-start.1 = (f32[1536]{0:T(1024)S(1)}, f32[1536]{0:T(1024)}, u32[]{:S(2)}) copy-start(f32[1536]{0:T(1024)} %g2.1) | copy-start | bytes 18436
  5.1 25.2 %copy-start.2 = (f32[1536]{0:T(1024)S(1)}, f32[1536]{0:T(1024)}, u32[]{:S(2)}) copy-start(f32[1536]{0:T(1024)} %b2.1) | copy-start | bytes 18436
  5.1 25.2 %copy-start.3 = (f32[1536]{0:T(1024)S(1)}, f32[1536]{0:T(1024)}, u32[]{:S(2)}) copy-start(f32[1536]{0:T(1024)} %g3.1) | copy-start | bytes 18436
  5.1 25.2 %copy-start.4 = (f32[1536]{0:T(1024)S(1)}, f32[1536]{0:T(1024)}, u32[]{:S(2)}) copy-start(f32[1536]{0:T(1024)} %b3.1) | copy-start | bytes 18436
where the time goes:
time: 57.8 us; the launch traced here: 57.6 us
  Pallas kernels  48.3 us (84%)
  waiting for transfers between devices  3.57 us (6%)
  starting transfers between devices  3.36 us (6%)
  local copies, waits for them, and re-layouts  1.07 us (2%)
  between operations  0.69 us (1%)
  other arithmetic  0.63 us (1%)
    pallas_call x1, Pallas kernels, local_step(): pl.pallas_call(functools.partial(rest_kernel, batch, heads, dim, tp), out...  26.7 us
    pallas_call x1, Pallas kernels, local_step(): pl.pallas_call(functools.partial(self_kernel, batch, heads, dim), out_sha...  21.6 us
    ppermute x1, waiting for transfers between devices, local_step(): wk_far = lax.ppermute(wk_c, 'tp', far)  3.57 us
    ppermute x1, starting transfers between devices, local_step(): wv_far = lax.ppermute(wv_cut, 'tp', far)  3.33 us
  transfers between devices with their start and end apart: 2, of which 1 were waited for; matrix products, arithmetic and copies ran while one was open for 0% of the time, Pallas kernels for 38%

commit v1 on v0

--- a/solution.py
+++ b/solution.py
@@ -198,13 +198,17 @@
 
 def rest_kernel(batch, heads, dim, tp, part_ref, x_ref, g2, b2, g3, b3, wqc_h, e_own_h, wk_h, wv_h, wkr_h, wvr_h, woc_h, wup_h, wdn_h,
                 out_ref,
-                wqc, enc, wkv, wkvr, woc, wup, wdn, kv_own, kv_rem, recv, send2, send3, qc_s, qc_r, o_snd, o_rcv,
-                lsem, ssem, rsem, xs, xr, ns, nr):
+                wqc, enc, wkv, wkvr, woc, wup, wdn, kv_own, kv_rem, v_late, near_1, far_2, sum_1, got_1, sum_2, got_2, send2, send3,
+                qc_s, qc_r, o_snd, o_rcv, o2_snd, o2_rcv, lsem, ssem, rsem, xs, xr, ns, nr):
     width = heads * dim
     scale = dim ** -0.5
+    d_model = part_ref.shape[1]
+    cut, quarter = d_model // 2, d_model // 4
     me = lax.axis_index('tp')
+    core = lax.rem(me, 2)
     far = lax.rem(me + 2, tp)
-    near = me + 1 - 2 * lax.rem(me, 2)
+    near = me + 1 - 2 * core
+    diag = lax.rem(near + 2, tp)
     half = enc.shape[0] // 2
     early = wvr_h.shape[1]
 
@@ -228,25 +232,42 @@
         pl.semaphore_signal(barrier, inc=1, device_id={'tp': lax.rem(me + d, tp)}, device_id_type=pl.DeviceIdType.MESH)
     pl.semaphore_wait(barrier, tp - 1)
 
-    def exchange(n, src):
-        for d in range(1, tp):
-            pltpu.make_async_remote_copy(src_ref=src, dst_ref=recv.at[n, me], send_sem=ssem.at[n, d - 1], recv_sem=rsem.at[n, me],
-                                         device_id={'tp': lax.rem(me + d, tp)}, device_id_type=pl.DeviceIdType.MESH).start()
-        recv[n, me] = src[...]
-
-    def collect(n, src):
-        for d in range(1, tp):
-            other = lax.rem(me + d, tp)
-            pltpu.make_async_remote_copy(src_ref=src, dst_ref=recv.at[n, other], send_sem=ssem.at[n, d - 1], recv_sem=rsem.at[n, other],
-                                         device_id={'tp': other}, device_id_type=pl.DeviceIdType.MESH).wait()
-        total = recv[n, 0].astype(F32)
-        for t in range(1, tp):
-            total = total + recv[n, t].astype(F32)
-        return total
-
-    def to_far(i, src, dst):
-        return pltpu.make_async_remote_copy(src_ref=src, dst_ref=dst, send_sem=xs.at[i], recv_sem=xr.at[i],
-                                            device_id={'tp': far}, device_id_type=pl.DeviceIdType.MESH)
+    def remote(src, dst, send_sem, recv_sem, device):
+        return pltpu.make_async_remote_copy(src_ref=src, dst_ref=dst, send_sem=send_sem, recv_sem=recv_sem,
+                                            device_id={'tp': device}, device_id_type=pl.DeviceIdType.MESH)
+
+    def far_copy(n, src):
+        return remote(src.at[:, pl.ds(cut, cut)], far_2.at[n], ssem.at[n, 1], rsem.at[n, 1], far)
+
+    def near_copy(n, src):
+        return remote(src.at[:, pl.ds(0, cut)], near_1.at[n], ssem.at[n, 0], rsem.at[n, 0], near)
+
+    def quarter_copies(n):
+        return [remote(sum_1.at[n, core], got_1.at[n, core], ssem.at[n, 2 + k], rsem.at[n, 2 + core], device) for k, device in enumerate((far, diag))]
+
+    def across_copy(n):
+        return remote(sum_2.at[n], got_2.at[n], ssem.at[n, 4], rsem.at[n, 4], near)
+
+    def pass_near(n, src):
+        near_copy(n, src).wait()
+        pair = (src[:, 0:cut].astype(F32) + near_1[n].astype(F32)).astype(BF16)
+        for k in range(2):
+            sum_1[n, k] = pair[:, k * quarter:(k + 1) * quarter]
+        for copy in quarter_copies(n):
+            copy.start()
+
+    def pass_far(n, src):
+        far_copy(n, src).wait()
+        sum_2[n] = (src[:, cut:].astype(F32) + far_2[n].astype(F32)).astype(BF16)
+        across_copy(n).start()
+
+    def total(n):
+        for copy in quarter_copies(n):
+            copy.wait_send()
+        for k in range(2):
+            remote(sum_1.at[n, k], got_1.at[n, k], ssem.at[n, 2], rsem.at[n, 2 + k], far).wait_recv()
+        across_copy(n).wait()
+        return jnp.concatenate([sum_1[n, k].astype(F32) + got_1[n, k].astype(F32) for k in range(2)] + [sum_2[n].astype(F32) + got_2[n].astype(F32)], axis=1)
 
     def project(first, count, jobs, tile=256):
         def body(i, c):
@@ -257,34 +278,56 @@
 
         lax.fori_loop(first // tile, (first + count) // tile, body, 0)
 
-    late_rows = (0, 640, wv_h.shape[0])
+    late_rows = (0, 512, wv_h.shape[0])
 
     def late(i):
         rows, cols = pl.ds(late_rows[i], late_rows[i + 1] - late_rows[i]), width - early
-        return to_far(2 + i, wv_h.at[rows, pl.ds(early, cols)], wkvr.at[rows, pl.ds(width + early, cols)])
-
-    exchange(0, part_ref)
-    near_e = pltpu.make_async_remote_copy(src_ref=e_own_h, dst_ref=enc.at[pl.ds(half, half), :], send_sem=ns.at[0], recv_sem=nr.at[0],
-                                          device_id={'tp': near}, device_id_type=pl.DeviceIdType.MESH)
-    near_e.start()
+        return remote(wv_h.at[rows, pl.ds(early, cols)], wkvr.at[rows, pl.ds(width + early, cols)], xs.at[3 + i], xr.at[3 + i], far)
+
+    def late_product(i, tile=256):
+        lo, hi = late_rows[i], late_rows[i + 1]
+
+        def body(t, c):
+            rows = pl.ds(pl.multiple_of(t * tile, tile), tile)
+            product = dot(enc[rows, lo:hi], wkvr[lo:hi, width + early:2 * width])
+            if i == 0:
+                v_late[rows, :] = product
+            else:
+                kv_rem[rows, width + early:2 * width] = (v_late[rows, :] + product).astype(BF16)
+            return c
+
+        lax.fori_loop(0, 2 * half // tile, body, 0)
+
+    def near_tokens(i):
+        rows = half // 2
+        return remote(e_own_h.at[pl.ds(i * rows, rows), :], enc.at[pl.ds(half + i * rows, rows), :], ns.at[i], nr.at[i], near)
+
+    own_job = (wkv, kv_own, 0, 2 * width)
+    far_job = (wkvr, kv_rem, 0, width + early)
+
+    far_copy(0, part_ref).start()
+    near_copy(0, part_ref).start()
+    near_tokens(0).start()
+    pass_near(0, part_ref)
     late(0).start()
-    jobs = ((wkv, kv_own, 0, 2 * width), (wkvr, kv_rem, 0, width + early))
     for copy in (ld_e0, ld_wk, ld_wv, ld_wkr, ld_wvr):
         copy.wait()
-    project(0, half, jobs)
-
-    h1 = x_ref[...].astype(F32) + collect(0, part_ref)
+    project(0, half // 2, (own_job, far_job))
+    pass_far(0, part_ref)
+    near_tokens(1).start()
+    project(half // 2, half // 2, (far_job,))
+    h1 = x_ref[...].astype(F32) + total(0)
     c_norm = layer_norm(h1, g2[...].reshape(1, -1), b2[...].reshape(1, -1))
     ld_wqc.wait()
     qc_s[...] = dot(c_norm, wqc[...]).astype(BF16)
-    send_q = to_far(0, qc_s, qc_r)
+    send_q = remote(qc_s, qc_r, xs.at[0], xr.at[0], far)
     send_q.start()
     late(1).start()
-    near_e.wait()
-    project(half, half, jobs[1:])
-    for i in range(2):
-        late(i).wait()
-    project(0, 2 * half, ((wkvr, kv_rem, width + early, 2 * width),))
+    near_tokens(0).wait()
+    near_tokens(1).wait()
+    project(half, half, (far_job,))
+    late(0).wait()
+    late_product(0)
 
     rows = heads * batch
     row_b = lax.rem(lax.broadcasted_iota(jnp.int32, (rows, 128), 0), batch)
@@ -296,7 +339,7 @@
     row_blk = row_b // pack
     lane_head = lax.broadcasted_iota(jnp.int32, (batch, width), 1) // dim
 
-    def attend(q, kv):
+    def weigh(q, kv):
         qf = q.astype(F32)
         q_rows = jnp.concatenate([jnp.where(lane_head == h, qf, 0.0) for h in range(heads)], axis=0).astype(BF16)
         parts = []
@@ -309,46 +352,61 @@
         m = jnp.maximum(jnp.max(parts[0], axis=1, keepdims=True), jnp.max(parts[1], axis=1, keepdims=True))
         p = [jnp.exp(s - m) for s in parts]
         l = jnp.sum(p[0], axis=1, keepdims=True) + jnp.sum(p[1], axis=1, keepdims=True)
-        o = None
-        for part in range(2):
-            p_wide = jnp.concatenate([jnp.where(row_blk == k, p[part], 0.0) for k in range(blocks)], axis=1).astype(BF16)
-            o_part = dot(p_wide, kv[part * half:(part + 1) * half, width:2 * width])
-            o = o_part if o is None else o + o_part
-        o = jnp.concatenate([o[h * batch:(h + 1) * batch, h * dim:(h + 1) * dim] for h in range(heads)], axis=0)
-        return m, l, o
-
+        wide = [jnp.concatenate([jnp.where(row_blk == k, p[part], 0.0) for k in range(blocks)], axis=1).astype(BF16) for part in range(2)]
+        return m, l, wide
+
+    def mix(wide, kv, first, last):
+        lo, hi = first * batch, last * batch
+        o = sum(dot(wide[part][lo:hi], kv[part * half:(part + 1) * half, width + first * dim:width + last * dim]) for part in range(2))
+        return jnp.concatenate([o[(h - first) * batch:(h - first + 1) * batch, (h - first) * dim:(h - first + 1) * dim] for h in range(first, last)], axis=0)
+
+    n_early = early // dim
     send_q.wait()
-    m_r, l_r, o_r = attend(qc_r[...], kv_rem)
-    o_snd[0:rows, :] = o_r
+    m_r, l_r, wide_r = weigh(qc_r[...], kv_rem)
+    o_snd[0:n_early * batch, :] = mix(wide_r, kv_rem, 0, n_early)
     stats = jnp.zeros((batch, dim), F32)
     st_lane = lax.broadcasted_iota(jnp.int32, (batch, dim), 1)
     for h in range(heads):
         stats = jnp.where(st_lane == 2 * h, m_r[h * batch:(h + 1) * batch], jnp.where(st_lane == 2 * h + 1, l_r[h * batch:(h + 1) * batch], stats))
-    o_snd[rows:rows + batch, :] = stats
-    send_o = to_far(1, o_snd, o_rcv)
+    o_snd[n_early * batch:(n_early + 1) * batch, :] = stats
+    send_o = remote(o_snd, o_rcv, xs.at[1], xr.at[1], far)
     send_o.start()
-    project(half, half, jobs[:1])
-    m_a, l_a, o_a = attend(qc_s[...], kv_own)
+    late(1).wait()
+    late_product(1)
+    o2_snd[...] = mix(wide_r, kv_rem, n_early, heads)
+    send_o2 = remote(o2_snd, o2_rcv, xs.at[2], xr.at[2], far)
+    send_o2.start()
+    project(half // 2, half // 2 + half, (own_job,))
+    m_a, l_a, wide_a = weigh(qc_s[...], kv_own)
+    o_a = mix(wide_a, kv_own, 0, heads)
     send_o.wait()
-    stats = o_rcv[rows:rows + batch, :]
+    stats = o_rcv[n_early * batch:(n_early + 1) * batch, :]
     m_b = jnp.concatenate([stats[:, 2 * h:2 * h + 1] for h in range(heads)], axis=0)
     l_b = jnp.concatenate([stats[:, 2 * h + 1:2 * h + 2] for h in range(heads)], axis=0)
     m = jnp.maximum(m_a, m_b)
     w_a, w_b = jnp.exp(m_a - m), jnp.exp(m_b - m)
-    o = (o_a * w_a + o_rcv[0:rows, :] * w_b) / (l_a * w_a + l_b * w_b)
+    send_o2.wait()
+    o_b = jnp.concatenate([o_rcv[0:n_early * batch, :], o2_rcv[...]], axis=0)
+    o = (o_a * w_a + o_b * w_b) / (l_a * w_a + l_b * w_b)
     oc = jnp.concatenate([o[h * batch:(h + 1) * batch, :] for h in range(heads)], axis=1).astype(BF16)
+
+    def matmul_sum(n, lhs, weights, out):
+        out[:, cut:] = dot(lhs, weights[:, cut:]).astype(BF16)
+        far_copy(n, out).start()
+        out[:, 0:cut] = dot(lhs, weights[:, 0:cut]).astype(BF16)
+        near_copy(n, out).start()
+        pass_near(n, out)
+        pass_far(n, out)
+        return total(n)
+
     ld_woc.wait()
-    send2[...] = dot(oc, woc[...]).astype(BF16)
-    exchange(1, send2)
-    h2 = h1 + collect(1, send2)
+    h2 = h1 + matmul_sum(1, oc, woc, send2)
     m_norm = layer_norm(h2, g3[...].reshape(1, -1), b3[...].reshape(1, -1))
     ld_up.wait()
     up = dot(m_norm, wup[...])
     hidden = (0.5 * up * (1.0 + lax.erf(up * (0.5 ** 0.5)))).astype(BF16)
     ld_dn.wait()
-    send3[...] = dot(hidden, wdn[...]).astype(BF16)
-    exchange(2, send3)
-    out_ref[...] = h2 + collect(2, send3)
+    out_ref[...] = h2 + matmul_sum(2, hidden, wdn, send3)
 
 
 def local_step(x, k_cache, v_cache, seq_lens, nbr_enc, ln1_gain, ln1_bias, w_q, w_k, w_v, w_o, ln2_gain, ln2_bias, wq_c, wk_c, wv_c, wo_c, ln3_gain, ln3_bias, w_up, w_down):
@@ -395,12 +453,15 @@
             pltpu.VMEM((d_model, width), BF16), pltpu.VMEM((2 * n_enc, enc_dim), BF16),
             pltpu.VMEM((enc_dim, 2 * width), BF16), pltpu.VMEM((enc_dim, 2 * width), BF16),
             pltpu.VMEM((width, d_model), BF16), pltpu.VMEM((d_model, ff), BF16), pltpu.VMEM((ff, d_model), BF16),
-            pltpu.VMEM((2 * n_enc, 2 * width), BF16), pltpu.VMEM((2 * n_enc, 2 * width), BF16),
-            pltpu.VMEM((3, tp, batch, d_model), BF16), pltpu.VMEM((batch, d_model), BF16), pltpu.VMEM((batch, d_model), BF16),
+            pltpu.VMEM((2 * n_enc, 2 * width), BF16), pltpu.VMEM((2 * n_enc, 2 * width), BF16), pltpu.VMEM((2 * n_enc, dim), F32),
+            pltpu.VMEM((3, batch, d_model // 2), BF16), pltpu.VMEM((3, batch, d_model // 2), BF16),
+            pltpu.VMEM((3, 2, batch, d_model // 4), BF16), pltpu.VMEM((3, 2, batch, d_model // 4), BF16),
+            pltpu.VMEM((3, batch, d_model // 2), BF16), pltpu.VMEM((3, batch, d_model // 2), BF16),
+            pltpu.VMEM((batch, d_model), BF16), pltpu.VMEM((batch, d_model), BF16),
             pltpu.VMEM((batch, width), BF16), pltpu.VMEM((batch, width), BF16),
-            pltpu.VMEM((heads * batch + batch, dim), F32), pltpu.VMEM((heads * batch + batch, dim), F32),
-            pltpu.SemaphoreType.DMA((9,)), pltpu.SemaphoreType.DMA((3, tp - 1)), pltpu.SemaphoreType.DMA((3, tp)),
-            pltpu.SemaphoreType.DMA((4,)), pltpu.SemaphoreType.DMA((4,)), pltpu.SemaphoreType.DMA((1,)), pltpu.SemaphoreType.DMA((1,)),
+            pltpu.VMEM((heads * batch, dim), F32), pltpu.VMEM((heads * batch, dim), F32), pltpu.VMEM((batch, dim), F32), pltpu.VMEM((batch, dim), F32),
+            pltpu.SemaphoreType.DMA((9,)), pltpu.SemaphoreType.DMA((3, 5)), pltpu.SemaphoreType.DMA((3, 5)),
+            pltpu.SemaphoreType.DMA((5,)), pltpu.SemaphoreType.DMA((5,)), pltpu.SemaphoreType.DMA((2,)), pltpu.SemaphoreType.DMA((2,)),
         ],
         compiler_params=pltpu.CompilerParams(collective_id=0, has_side_effects=True, vmem_limit_bytes=46000000),
         cost_estimate=pl.CostEstimate(flops=20_000_000_000, bytes_accessed=30_000_000, transcendentals=0),

time: 57.8 us -> 60.1 us (1.040)
  Pallas kernels: 48.3 us -> 50.7 us
    pallas_call x1, Pallas kernels: 26.7 us -> 29 us  [local_step(): pl.pallas_call(functools.partial(rest_kernel, batch, heads, dim, tp), out...]
  transfers between devices with their start and end apart: 2 -> 2, of which waited for: 1 -> 1; matrix products, arithmetic and copies ran while one was open for 0% -> 0% of each run, Pallas kernels for 38% -> 36%
where the time goes in v1:
time: 60.1 us; the launch traced here: 60 us
  Pallas kernels  50.7 us (84%)
  waiting for transfers between devices  3.57 us (6%)
  starting transfers between devices  3.36 us (6%)
  local copies, waits for them, and re-layouts  1.07 us (2%)
  between operations  0.69 us (1%)
  other arithmetic  0.63 us (1%)
    pallas_call x1, Pallas kernels, local_step(): pl.pallas_call(functools.partial(rest_kernel, batch, heads, dim, tp), out...  29 us
    pallas_call x1, Pallas kernels, local_step(): pl.pallas_call(functools.partial(self_kernel, batch, heads, dim), out_sha...  21.6 us
    ppermute x1, waiting for transfers between devices, local_step(): wk_far = lax.ppermute(wk_c, 'tp', far)  3.57 us
    ppermute x1, starting transfers between devices, local_step(): wv_far = lax.ppermute(wv_cut, 'tp', far)  3.33 us
  transfers between devices with their start and end apart: 2, of which 1 were waited for; matrix products, arithmetic and copies ran while one was open for 0% of the time, Pallas kernels for 36%

profile of v1, /device:TPU:0, one launch (start us, length us, event | category | flops | bytes accessed | tf_op | source)
XLA Modules:
  0.0 60.0 jit_solution(2779433264431301610)
XLA Ops:
  0.6 1.1 %slice.3 = bf16[896,256]{1,0:T(8,128)(2,1)S(1)} slice(bf16[896,384]{1,0:T(8,128)(2,1)} %wv_h.3), slice={[0:896], [0:256]} | slice | bytes 917504 | tf_op jit(solution)/shard_map/slice | solution.py:420
  1.7 3.3 %collective-permute-start.1 = (bf16[896,256]{1,0:T(8,128)(2,1)S(1)}, bf16[896,256]{1,0:T(8,128)(2,1)S(1)}, u32[]{:S(2)}, u32[]{:S(2)}) collective-permute-start(bf16[896,256]{1,0:T(8,128)(2,1)S(1)} %slice.3), channel_id=1, source_target_pairs={{0,2},{1,3},{2,0},{3,1},{4,6},{5,7},{6,4},{7,5}} | collective-permute-start | bytes 1376264 | tf_op jit(solution)/shard_map/ppermute | solution.py:421
  5.0 0.0 collective-permute-start
  5.0 0.0 copy-start
  5.0 0.0 copy-start.1
  5.1 0.0 copy-start.2
  5.1 0.0 copy-start.3
  5.1 0.0 copy-start.4
  5.1 21.6 %self_attention.1 = (bf16[16,1536]{1,0:T(8,128)(2,1)S(1)}, bf16[3,16,128]{2,1,0:T(8,128)(2,1)}, bf16[3,16,128]{2,1,0:T(8,128)(2,1)}) custom-call(s32[16]{0:T(128)} %lens_h.1, bf16[16,1536]{1,0:T(8,128)(2,1)} %x_ref.1, f32[1536]{0:T(1024)} %g_h.1, f32[1536]{0:T(1024)} %b_h.1, bf16[16,3,4096,128]{3,2,1,0:T(8,128)(2,1)} %bitcast.5, ...), custom_call_target="tpu_custom_call" | custom-call | flops 40000000000 | bytes 60000000 | tf_op jit(solution)/shard_map/self_attention/pallas_call | solution.py:427
  26.7 0.0 collective-permute-done.1.wvr_h
  26.7 3.6 %collective-permute-done.wkr_h = bf16[896,384]{1,0:T(8,128)(2,1)S(1)} collective-permute-done((bf16[896,384]{1,0:T(8,128)(2,1)}, bf16[896,384]{1,0:T(8,128)(2,1)S(1)}, u32[]{:S(2)}, u32[]{:S(2)}) %collective-permute-start) | collective-permute-done | bytes 688160 | tf_op jit(solution)/shard_map/ppermute | solution.py:419
  30.3 0.0 copy-done
  30.3 0.0 copy-done.1
  30.3 0.0 copy-done.2
  30.3 0.0 copy-done.3
  30.3 0.0 copy-done.4
  30.3 29.0 %rest_of_layer.1 = f32[16,1536]{1,0:T(8,128)S(1)} custom-call(bf16[16,1536]{1,0:T(8,128)(2,1)S(1)} %get-tuple-element.6.part_ref, bf16[16,1536]{1,0:T(8,128)(2,1)S(1)} %copy-done, f32[1536]{0:T(1024)S(1)} %copy-done.1, f32[1536]{0:T(1024)S(1)} %copy-done.2, f32[1536]{0:T(1024)S(1)} %copy-done.3, f32[1536]{0:T(1024)S(1)} %copy-done.4, ...), custom_call_target="tpu_custom_call" | custom-call | flops 20000000000 | bytes 30000000 | tf_op jit(solution)/shard_map/rest_of_layer/pallas_call | solution.py:447
  59.4 0.6 %convert_element_type.3 = bf16[16,1536]{1,0:T(8,128)(2,1)} convert(f32[16,1536]{1,0:T(8,128)S(1)} %rest_of_layer.1) | non-fusion elementwise | flops 24576 | bytes 147456 | tf_op jit(solution)/shard_map/convert_element_type | solution.py:470
Async XLA Ops:
  1.7 25.0 %collective-permute-start.1 = (bf16[896,256]{1,0:T(8,128)(2,1)S(1)}, bf16[896,256]{1,0:T(8,128)(2,1)S(1)}, u32[]{:S(2)}, u32[]{:S(2)}) collective-permute-start(bf16[896,256]{1,0:T(8,128)(2,1)S(1)} %slice.3), channel_id=1, source_target_pairs={{0,2},{1,3},{2,0},{3,1},{4,6},{5,7},{6,4},{7,5}} | collective-permute-start | bytes 1376264 | tf_op jit(solution)/shard_map/ppermute | solution.py:421
  5.0 25.3 %collective-permute-start = (bf16[896,384]{1,0:T(8,128)(2,1)}, bf16[896,384]{1,0:T(8,128)(2,1)S(1)}, u32[]{:S(2)}, u32[]{:S(2)}) collective-permute-start(bf16[896,384]{1,0:T(8,128)(2,1)} %wk_h.3), channel_id=1, source_target_pairs={{0,2},{1,3},{2,0},{3,1},{4,6},{5,7},{6,4},{7,5}} | collective-permute-start | bytes 2064392 | tf_op jit(solution)/shard_map/ppermute | solution.py:419
  5.0 25.2 %copy-start = (bf16[16,1536]{1,0:T(8,128)(2,1)S(1)}, bf16[16,1536]{1,0:T(8,128)(2,1)}, u32[]{:S(2)}) copy-start(bf16[16,1536]{1,0:T(8,128)(2,1)} %x_ref.1) | copy-start | bytes 147460
  5.0 25.2 %copy-start.1 = (f32[1536]{0:T(1024)S(1)}, f32[1536]{0:T(1024)}, u32[]{:S(2)}) copy-start(f32[1536]{0:T(1024)} %g2.1) | copy-start | bytes 18436
  5.1 25.2 %copy-start.2 = (f32[1536]{0:T(1024)S(1)}, f32[1536]{0:T(1024)}, u32[]{:S(2)}) copy-start(f32[1536]{0:T(1024)} %b2.1) | copy-start | bytes 18436
  5.1 25.2 %copy-start.3 = (f32[1536]{0:T(1024)S(1)}, f32[1536]{0:T(1024)}, u32[]{:S(2)}) copy-start(f32[1536]{0:T(1024)} %g3.1) | copy-start | bytes 18436
  5.1 25.2 %copy-start.4 = (f32[1536]{0:T(1024)S(1)}, f32[1536]{0:T(1024)}, u32[]{:S(2)}) copy-start(f32[1536]{0:T(1024)} %b3.1) | copy-start | bytes 18436

commit v2 on v1

--- a/solution.py
+++ b/solution.py
@@ -198,17 +198,13 @@
 
 def rest_kernel(batch, heads, dim, tp, part_ref, x_ref, g2, b2, g3, b3, wqc_h, e_own_h, wk_h, wv_h, wkr_h, wvr_h, woc_h, wup_h, wdn_h,
                 out_ref,
-                wqc, enc, wkv, wkvr, woc, wup, wdn, kv_own, kv_rem, v_late, near_1, far_2, sum_1, got_1, sum_2, got_2, send2, send3,
+                wqc, enc, wkv, wkvr, woc, wup, wdn, kv_own, kv_rem, v_late, recv, send2, send3,
                 qc_s, qc_r, o_snd, o_rcv, o2_snd, o2_rcv, lsem, ssem, rsem, xs, xr, ns, nr):
     width = heads * dim
     scale = dim ** -0.5
-    d_model = part_ref.shape[1]
-    cut, quarter = d_model // 2, d_model // 4
     me = lax.axis_index('tp')
-    core = lax.rem(me, 2)
     far = lax.rem(me + 2, tp)
-    near = me + 1 - 2 * core
-    diag = lax.rem(near + 2, tp)
+    near = me + 1 - 2 * lax.rem(me, 2)
     half = enc.shape[0] // 2
     early = wvr_h.shape[1]
 
@@ -236,38 +232,24 @@
         return pltpu.make_async_remote_copy(src_ref=src, dst_ref=dst, send_sem=send_sem, recv_sem=recv_sem,
                                             device_id={'tp': device}, device_id_type=pl.DeviceIdType.MESH)
 
-    def far_copy(n, src):
-        return remote(src.at[:, pl.ds(cut, cut)], far_2.at[n], ssem.at[n, 1], rsem.at[n, 1], far)
-
-    def near_copy(n, src):
-        return remote(src.at[:, pl.ds(0, cut)], near_1.at[n], ssem.at[n, 0], rsem.at[n, 0], near)
-
-    def quarter_copies(n):
-        return [remote(sum_1.at[n, core], got_1.at[n, core], ssem.at[n, 2 + k], rsem.at[n, 2 + core], device) for k, device in enumerate((far, diag))]
-
-    def across_copy(n):
-        return remote(sum_2.at[n], got_2.at[n], ssem.at[n, 4], rsem.at[n, 4], near)
-
-    def pass_near(n, src):
-        near_copy(n, src).wait()
-        pair = (src[:, 0:cut].astype(F32) + near_1[n].astype(F32)).astype(BF16)
-        for k in range(2):
-            sum_1[n, k] = pair[:, k * quarter:(k + 1) * quarter]
-        for copy in quarter_copies(n):
+    def sum_copies(n, src):
+        return [remote(src, recv.at[n, me], ssem.at[n, d - 1], rsem.at[n, me], lax.rem(me + d, tp)) for d in range(1, tp)]
+
+    def exchange(n, src):
+        for copy in sum_copies(n, src):
             copy.start()
-
-    def pass_far(n, src):
-        far_copy(n, src).wait()
-        sum_2[n] = (src[:, cut:].astype(F32) + far_2[n].astype(F32)).astype(BF16)
-        across_copy(n).start()
-
-    def total(n):
-        for copy in quarter_copies(n):
+        recv[n, me] = src[...]
+
+    def collect(n, src):
+        for copy in sum_copies(n, src):
             copy.wait_send()
-        for k in range(2):
-            remote(sum_1.at[n, k], got_1.at[n, k], ssem.at[n, 2], rsem.at[n, 2 + k], far).wait_recv()
-        across_copy(n).wait()
-        return jnp.concatenate([sum_1[n, k].astype(F32) + got_1[n, k].astype(F32) for k in range(2)] + [sum_2[n].astype(F32) + got_2[n].astype(F32)], axis=1)
+        for d in range(1, tp):
+            other = lax.rem(me + d, tp)
+            remote(src, recv.at[n, other], ssem.at[n, d - 1], rsem.at[n, other], other).wait_recv()
+        total = recv[n, 0].astype(F32)
+        for t in range(1, tp):
+            total = total + recv[n, t].astype(F32)
+        return total
 
     def project(first, count, jobs, tile=256):
         def body(i, c):
@@ -305,18 +287,14 @@
     own_job = (wkv, kv_own, 0, 2 * width)
     far_job = (wkvr, kv_rem, 0, width + early)
 
-    far_copy(0, part_ref).start()
-    near_copy(0, part_ref).start()
+    exchange(0, part_ref)
     near_tokens(0).start()
-    pass_near(0, part_ref)
+    near_tokens(1).start()
     late(0).start()
     for copy in (ld_e0, ld_wk, ld_wv, ld_wkr, ld_wvr):
         copy.wait()
-    project(0, half // 2, (own_job, far_job))
-    pass_far(0, part_ref)
-    near_tokens(1).start()
-    project(half // 2, half // 2, (far_job,))
-    h1 = x_ref[...].astype(F32) + total(0)
+    project(0, half, (own_job, far_job))
+    h1 = x_ref[...].astype(F32) + collect(0, part_ref)
     c_norm = layer_norm(h1, g2[...].reshape(1, -1), b2[...].reshape(1, -1))
     ld_wqc.wait()
     qc_s[...] = dot(c_norm, wqc[...]).astype(BF16)
@@ -376,7 +354,7 @@
     o2_snd[...] = mix(wide_r, kv_rem, n_early, heads)
     send_o2 = remote(o2_snd, o2_rcv, xs.at[2], xr.at[2], far)
     send_o2.start()
-    project(half // 2, half // 2 + half, (own_job,))
+    project(half, half, (own_job,))
     m_a, l_a, wide_a = weigh(qc_s[...], kv_own)
     o_a = mix(wide_a, kv_own, 0, heads)
     send_o.wait()
@@ -391,13 +369,9 @@
     oc = jnp.concatenate([o[h * batch:(h + 1) * batch, :] for h in range(heads)], axis=1).astype(BF16)
 
     def matmul_sum(n, lhs, weights, out):
-        out[:, cut:] = dot(lhs, weights[:, cut:]).astype(BF16)
-        far_copy(n, out).start()
-        out[:, 0:cut] = dot(lhs, weights[:, 0:cut]).astype(BF16)
-        near_copy(n, out).start()
-        pass_near(n, out)
-        pass_far(n, out)
-        return total(n)
+        out[...] = dot(lhs, weights[...]).astype(BF16)
+        exchange(n, out)
+        return collect(n, out)
 
     ld_woc.wait()
     h2 = h1 + matmul_sum(1, oc, woc, send2)
@@ -454,13 +428,11 @@
             pltpu.VMEM((enc_dim, 2 * width), BF16), pltpu.VMEM((enc_dim, 2 * width), BF16),
             pltpu.VMEM((width, d_model), BF16), pltpu.VMEM((d_model, ff), BF16), pltpu.VMEM((ff, d_model), BF16),
             pltpu.VMEM((2 * n_enc, 2 * width), BF16), pltpu.VMEM((2 * n_enc, 2 * width), BF16), pltpu.VMEM((2 * n_enc, dim), F32),
-            pltpu.VMEM((3, batch, d_model // 2), BF16), pltpu.VMEM((3, batch, d_model // 2), BF16),
-            pltpu.VMEM((3, 2, batch, d_model // 4), BF16), pltpu.VMEM((3, 2, batch, d_model // 4), BF16),
-            pltpu.VMEM((3, batch, d_model // 2), BF16), pltpu.VMEM((3, batch, d_model // 2), BF16),
+            pltpu.VMEM((3, tp, batch, d_model), BF16),
             pltpu.VMEM((batch, d_model), BF16), pltpu.VMEM((batch, d_model), BF16),
             pltpu.VMEM((batch, width), BF16), pltpu.VMEM((batch, width), BF16),
             pltpu.VMEM((heads * batch, dim), F32), pltpu.VMEM((heads * batch, dim), F32), pltpu.VMEM((batch, dim), F32), pltpu.VMEM((batch, dim), F32),
-            pltpu.SemaphoreType.DMA((9,)), pltpu.SemaphoreType.DMA((3, 5)), pltpu.SemaphoreType.DMA((3, 5)),
+            pltpu.SemaphoreType.DMA((9,)), pltpu.SemaphoreType.DMA((3, tp - 1)), pltpu.SemaphoreType.DMA((3, tp)),
             pltpu.SemaphoreType.DMA((5,)), pltpu.SemaphoreType.DMA((5,)), pltpu.SemaphoreType.DMA((2,)), pltpu.SemaphoreType.DMA((2,)),
         ],
         compiler_params=pltpu.CompilerParams(collective_id=0, has_side_effects=True, vmem_limit_bytes=46000000),

time: 60.1 us -> 57.5 us (0.957)
  Pallas kernels: 50.7 us -> 48 us
    pallas_call x1, Pallas kernels: 29 us -> 26.4 us  [local_step(): pl.pallas_call(functools.partial(rest_kernel, batch, heads, dim, tp), out...]
  transfers between devices with their start and end apart: 2 -> 2, of which waited for: 1 -> 1; matrix products, arithmetic and copies ran while one was open for 0% -> 0% of each run, Pallas kernels for 36% -> 38%
where the time goes in v2:
time: 57.5 us; the launch traced here: 57.3 us
  Pallas kernels  48 us (83%)
  waiting for transfers between devices  3.57 us (6%)
  starting transfers between devices  3.36 us (6%)
  local copies, waits for them, and re-layouts  1.07 us (2%)
  between operations  0.69 us (1%)
  other arithmetic  0.63 us (1%)
    pallas_call x1, Pallas kernels, local_step(): pl.pallas_call(functools.partial(rest_kernel, batch, heads, dim, tp), out...  26.4 us
    pallas_call x1, Pallas kernels, local_step(): pl.pallas_call(functools.partial(self_kernel, batch, heads, dim), out_sha...  21.6 us
    ppermute x1, waiting for transfers between devices, local_step(): wk_far = lax.ppermute(wk_c, 'tp', far)  3.57 us
    ppermute x1, starting transfers between devices, local_step(): wv_far = lax.ppermute(wv_cut, 'tp', far)  3.33 us
  transfers between devices with their start and end apart: 2, of which 1 were waited for; matrix products, arithmetic and copies ran while one was open for 0% of the time, Pallas kernels for 38%

profile of v2, /device:TPU:0, one launch (start us, length us, event | category | flops | bytes accessed | tf_op | source)
XLA Modules:
  0.0 57.3 jit_solution(12421202850863426700)
XLA Ops:
  0.6 1.1 %slice.3 = bf16[896,256]{1,0:T(8,128)(2,1)S(1)} slice(bf16[896,384]{1,0:T(8,128)(2,1)} %wv_h.3), slice={[0:896], [0:256]} | slice | bytes 917504 | tf_op jit(solution)/shard_map/slice | solution.py:394
  1.7 3.3 %collective-permute-start.1 = (bf16[896,256]{1,0:T(8,128)(2,1)S(1)}, bf16[896,256]{1,0:T(8,128)(2,1)S(1)}, u32[]{:S(2)}, u32[]{:S(2)}) collective-permute-start(bf16[896,256]{1,0:T(8,128)(2,1)S(1)} %slice.3), channel_id=1, source_target_pairs={{0,2},{1,3},{2,0},{3,1},{4,6},{5,7},{6,4},{7,5}} | collective-permute-start | bytes 1376264 | tf_op jit(solution)/shard_map/ppermute | solution.py:395
  5.0 0.0 collective-permute-start
  5.0 0.0 copy-start
  5.0 0.0 copy-start.1
  5.1 0.0 copy-start.2
  5.1 0.0 copy-start.3
  5.1 0.0 copy-start.4
  5.1 21.6 %self_attention.1 = (bf16[16,1536]{1,0:T(8,128)(2,1)S(1)}, bf16[3,16,128]{2,1,0:T(8,128)(2,1)}, bf16[3,16,128]{2,1,0:T(8,128)(2,1)}) custom-call(s32[16]{0:T(128)} %lens_h.1, bf16[16,1536]{1,0:T(8,128)(2,1)} %x_ref.1, f32[1536]{0:T(1024)} %g_h.1, f32[1536]{0:T(1024)} %b_h.1, bf16[16,3,4096,128]{3,2,1,0:T(8,128)(2,1)} %bitcast.5, ...), custom_call_target="tpu_custom_call" | custom-call | flops 40000000000 | bytes 60000000 | tf_op jit(solution)/shard_map/self_attention/pallas_call | solution.py:401
  26.7 0.0 collective-permute-done.1.wvr_h
  26.7 3.6 %collective-permute-done.wkr_h = bf16[896,384]{1,0:T(8,128)(2,1)S(1)} collective-permute-done((bf16[896,384]{1,0:T(8,128)(2,1)}, bf16[896,384]{1,0:T(8,128)(2,1)S(1)}, u32[]{:S(2)}, u32[]{:S(2)}) %collective-permute-start) | collective-permute-done | bytes 688160 | tf_op jit(solution)/shard_map/ppermute | solution.py:393
  30.3 0.0 copy-done
  30.3 0.0 copy-done.1
  30.3 0.0 copy-done.2
  30.3 0.0 copy-done.3
  30.3 0.0 copy-done.4
  30.3 26.4 %rest_of_layer.1 = f32[16,1536]{1,0:T(8,128)S(1)} custom-call(bf16[16,1536]{1,0:T(8,128)(2,1)S(1)} %get-tuple-element.6.part_ref, bf16[16,1536]{1,0:T(8,128)(2,1)S(1)} %copy-done, f32[1536]{0:T(1024)S(1)} %copy-done.1, f32[1536]{0:T(1024)S(1)} %copy-done.2, f32[1536]{0:T(1024)S(1)} %copy-done.3, f32[1536]{0:T(1024)S(1)} %copy-done.4, ...), custom_call_target="tpu_custom_call" | custom-call | flops 20000000000 | bytes 30000000 | tf_op jit(solution)/shard_map/rest_of_layer/pallas_call | solution.py:421
  56.7 0.6 %convert_element_type.3 = bf16[16,1536]{1,0:T(8,128)(2,1)} convert(f32[16,1536]{1,0:T(8,128)S(1)} %rest_of_layer.1) | non-fusion elementwise | flops 24576 | bytes 147456 | tf_op jit(solution)/shard_map/convert_element_type | solution.py:442
Async XLA Ops:
  1.7 25.0 %collective-permute-start.1 = (bf16[896,256]{1,0:T(8,128)(2,1)S(1)}, bf16[896,256]{1,0:T(8,128)(2,1)S(1)}, u32[]{:S(2)}, u32[]{:S(2)}) collective-permute-start(bf16[896,256]{1,0:T(8,128)(2,1)S(1)} %slice.3), channel_id=1, source_target_pairs={{0,2},{1,3},{2,0},{3,1},{4,6},{5,7},{6,4},{7,5}} | collective-permute-start | bytes 1376264 | tf_op jit(solution)/shard_map/ppermute | solution.py:395
  5.0 25.3 %collective-permute-start = (bf16[896,384]{1,0:T(8,128)(2,1)}, bf16[896,384]{1,0:T(8,128)(2,1)S(1)}, u32[]{:S(2)}, u32[]{:S(2)}) collective-permute-start(bf16[896,384]{1,0:T(8,128)(2,1)} %wk_h.3), channel_id=1, source_target_pairs={{0,2},{1,3},{2,0},{3,1},{4,6},{5,7},{6,4},{7,5}} | collective-permute-start | bytes 2064392 | tf_op jit(solution)/shard_map/ppermute | solution.py:393
  5.0 25.2 %copy-start = (bf16[16,1536]{1,0:T(8,128)(2,1)S(1)}, bf16[16,1536]{1,0:T(8,128)(2,1)}, u32[]{:S(2)}) copy-start(bf16[16,1536]{1,0:T(8,128)(2,1)} %x_ref.1) | copy-start | bytes 147460
  5.0 25.2 %copy-start.1 = (f32[1536]{0:T(1024)S(1)}, f32[1536]{0:T(1024)}, u32[]{:S(2)}) copy-start(f32[1536]{0:T(1024)} %g2.1) | copy-start | bytes 18436
  5.1 25.2 %copy-start.2 = (f32[1536]{0:T(1024)S(1)}, f32[1536]{0:T(1024)}, u32[]{:S(2)}) copy-start(f32[1536]{0:T(1024)} %b2.1) | copy-start | bytes 18436
  5.1 25.2 %copy-start.3 = (f32[1536]{0:T(1024)S(1)}, f32[1536]{0:T(1024)}, u32[]{:S(2)}) copy-start(f32[1536]{0:T(1024)} %g3.1) | copy-start | bytes 18436
  5.1 25.2 %copy-start.4 = (f32[1536]{0:T(1024)S(1)}, f32[1536]{0:T(1024)}, u32[]{:S(2)}) copy-start(f32[1536]{0:T(1024)} %b3.1) | copy-start | bytes 18436

commit v3 on v2

--- a/solution.py
+++ b/solution.py
@@ -16,6 +16,7 @@
 UNROLL = 4
 GRAIN = 64
 GROUPS = 6
+PIECES = 3
 
 
 def layer_norm(values, ln_gain, ln_bias):
@@ -198,8 +199,8 @@
 
 def rest_kernel(batch, heads, dim, tp, part_ref, x_ref, g2, b2, g3, b3, wqc_h, e_own_h, wk_h, wv_h, wkr_h, wvr_h, woc_h, wup_h, wdn_h,
                 out_ref,
-                wqc, enc, wkv, wkvr, woc, wup, wdn, kv_own, kv_rem, v_late, recv, send2, send3,
-                qc_s, qc_r, o_snd, o_rcv, o2_snd, o2_rcv, lsem, ssem, rsem, xs, xr, ns, nr):
+                wqc, enc, wkv, wkvr, woc, wup, wdn, kv_own, kv_rem, v_late, recv1, recv, send2, send3,
+                qc_s, qc_r, o_snd, o_rcv, o2_snd, o2_rcv, lsem, ssem1, rsem1, ssem, rsem, xs, xr, ns, nr):
     width = heads * dim
     scale = dim ** -0.5
     me = lax.axis_index('tp')
@@ -232,8 +233,10 @@
         return pltpu.make_async_remote_copy(src_ref=src, dst_ref=dst, send_sem=send_sem, recv_sem=recv_sem,
                                             device_id={'tp': device}, device_id_type=pl.DeviceIdType.MESH)
 
+    others = [lax.rem(me + d, tp) for d in (2, 3, 1)]
+
     def sum_copies(n, src):
-        return [remote(src, recv.at[n, me], ssem.at[n, d - 1], rsem.at[n, me], lax.rem(me + d, tp)) for d in range(1, tp)]
+        return [remote(src, recv.at[n, me], ssem.at[n, k], rsem.at[n, me], device) for k, device in enumerate(others)]
 
     def exchange(n, src):
         for copy in sum_copies(n, src):
@@ -243,13 +246,19 @@
     def collect(n, src):
         for copy in sum_copies(n, src):
             copy.wait_send()
-        for d in range(1, tp):
-            other = lax.rem(me + d, tp)
-            remote(src, recv.at[n, other], ssem.at[n, d - 1], rsem.at[n, other], other).wait_recv()
+        for k, device in enumerate(others):
+            remote(src, recv.at[n, device], ssem.at[n, k], rsem.at[n, device], device).wait_recv()
         total = recv[n, 0].astype(F32)
         for t in range(1, tp):
             total = total + recv[n, t].astype(F32)
         return total
+
+    def matmul_sum(n, lhs, weights, send):
+        size = send.shape[2]
+        for k in range(send.shape[0]):
+            send[k] = dot(lhs, weights[:, k * size:(k + 1) * size]).astype(BF16)
+            exchange(n + k, send.at[k])
+        return jnp.concatenate([collect(n + k, send.at[k]) for k in range(send.shape[0])], axis=1)
 
     def project(first, count, jobs, tile=256):
         def body(i, c):
@@ -260,7 +269,7 @@
 
         lax.fori_loop(first // tile, (first + count) // tile, body, 0)
 
-    late_rows = (0, 512, wv_h.shape[0])
+    late_rows = (0, 256, 640, wv_h.shape[0])
 
     def late(i):
         rows, cols = pl.ds(late_rows[i], late_rows[i + 1] - late_rows[i]), width - early
@@ -274,6 +283,8 @@
             product = dot(enc[rows, lo:hi], wkvr[lo:hi, width + early:2 * width])
             if i == 0:
                 v_late[rows, :] = product
+            elif i + 2 < len(late_rows):
+                v_late[rows, :] = v_late[rows, :] + product
             else:
                 kv_rem[rows, width + early:2 * width] = (v_late[rows, :] + product).astype(BF16)
             return c
@@ -287,20 +298,29 @@
     own_job = (wkv, kv_own, 0, 2 * width)
     far_job = (wkvr, kv_rem, 0, width + early)
 
-    exchange(0, part_ref)
+    first_copies = [remote(part_ref, recv1.at[me], ssem1.at[k], rsem1.at[me], device) for k, device in enumerate(others)]
+    for copy in first_copies:
+        copy.start()
+    recv1[me] = part_ref[...]
     near_tokens(0).start()
     near_tokens(1).start()
     late(0).start()
     for copy in (ld_e0, ld_wk, ld_wv, ld_wkr, ld_wvr):
         copy.wait()
     project(0, half, (own_job, far_job))
-    h1 = x_ref[...].astype(F32) + collect(0, part_ref)
+    for copy in first_copies:
+        copy.wait_send()
+    for k, device in enumerate(others):
+        remote(part_ref, recv1.at[device], ssem1.at[k], rsem1.at[device], device).wait_recv()
+    h1 = x_ref[...].astype(F32)
+    h1 = h1 + sum((recv1[t].astype(F32) for t in range(1, tp)), recv1[0].astype(F32))
     c_norm = layer_norm(h1, g2[...].reshape(1, -1), b2[...].reshape(1, -1))
     ld_wqc.wait()
     qc_s[...] = dot(c_norm, wqc[...]).astype(BF16)
     send_q = remote(qc_s, qc_r, xs.at[0], xr.at[0], far)
     send_q.start()
     late(1).start()
+    late(2).start()
     near_tokens(0).wait()
     near_tokens(1).wait()
     project(half, half, (far_job,))
@@ -349,8 +369,9 @@
     o_snd[n_early * batch:(n_early + 1) * batch, :] = stats
     send_o = remote(o_snd, o_rcv, xs.at[1], xr.at[1], far)
     send_o.start()
-    late(1).wait()
-    late_product(1)
+    for i in (1, 2):
+        late(i).wait()
+        late_product(i)
     o2_snd[...] = mix(wide_r, kv_rem, n_early, heads)
     send_o2 = remote(o2_snd, o2_rcv, xs.at[2], xr.at[2], far)
     send_o2.start()
@@ -368,19 +389,14 @@
     o = (o_a * w_a + o_b * w_b) / (l_a * w_a + l_b * w_b)
     oc = jnp.concatenate([o[h * batch:(h + 1) * batch, :] for h in range(heads)], axis=1).astype(BF16)
 
-    def matmul_sum(n, lhs, weights, out):
-        out[...] = dot(lhs, weights[...]).astype(BF16)
-        exchange(n, out)
-        return collect(n, out)
-
     ld_woc.wait()
-    h2 = h1 + matmul_sum(1, oc, woc, send2)
+    h2 = h1 + matmul_sum(0, oc, woc, send2)
     m_norm = layer_norm(h2, g3[...].reshape(1, -1), b3[...].reshape(1, -1))
     ld_up.wait()
     up = dot(m_norm, wup[...])
     hidden = (0.5 * up * (1.0 + lax.erf(up * (0.5 ** 0.5)))).astype(BF16)
     ld_dn.wait()
-    out_ref[...] = h2 + matmul_sum(2, hidden, wdn, send3)
+    out_ref[...] = h2 + matmul_sum(send2.shape[0], hidden, wdn, send3)
 
 
 def local_step(x, k_cache, v_cache, seq_lens, nbr_enc, ln1_gain, ln1_bias, w_q, w_k, w_v, w_o, ln2_gain, ln2_bias, wq_c, wk_c, wv_c, wo_c, ln3_gain, ln3_bias, w_up, w_down):
@@ -428,12 +444,13 @@
             pltpu.VMEM((enc_dim, 2 * width), BF16), pltpu.VMEM((enc_dim, 2 * width), BF16),
             pltpu.VMEM((width, d_model), BF16), pltpu.VMEM((d_model, ff), BF16), pltpu.VMEM((ff, d_model), BF16),
             pltpu.VMEM((2 * n_enc, 2 * width), BF16), pltpu.VMEM((2 * n_enc, 2 * width), BF16), pltpu.VMEM((2 * n_enc, dim), F32),
-            pltpu.VMEM((3, tp, batch, d_model), BF16),
-            pltpu.VMEM((batch, d_model), BF16), pltpu.VMEM((batch, d_model), BF16),
+            pltpu.VMEM((tp, batch, d_model), BF16), pltpu.VMEM((2 * PIECES, tp, batch, d_model // PIECES), BF16),
+            pltpu.VMEM((PIECES, batch, d_model // PIECES), BF16), pltpu.VMEM((PIECES, batch, d_model // PIECES), BF16),
             pltpu.VMEM((batch, width), BF16), pltpu.VMEM((batch, width), BF16),
             pltpu.VMEM((heads * batch, dim), F32), pltpu.VMEM((heads * batch, dim), F32), pltpu.VMEM((batch, dim), F32), pltpu.VMEM((batch, dim), F32),
-            pltpu.SemaphoreType.DMA((9,)), pltpu.SemaphoreType.DMA((3, tp - 1)), pltpu.SemaphoreType.DMA((3, tp)),
-            pltpu.SemaphoreType.DMA((5,)), pltpu.SemaphoreType.DMA((5,)), pltpu.SemaphoreType.DMA((2,)), pltpu.SemaphoreType.DMA((2,)),
+            pltpu.SemaphoreType.DMA((9,)), pltpu.SemaphoreType.DMA((tp - 1,)), pltpu.SemaphoreType.DMA((tp,)),
+            pltpu.SemaphoreType.DMA((2 * PIECES, tp - 1)), pltpu.SemaphoreType.DMA((2 * PIECES, tp)),
+            pltpu.SemaphoreType.DMA((6,)), pltpu.SemaphoreType.DMA((6,)), pltpu.SemaphoreType.DMA((2,)), pltpu.SemaphoreType.DMA((2,)),
         ],
         compiler_params=pltpu.CompilerParams(collective_id=0, has_side_effects=True, vmem_limit_bytes=46000000),
         cost_estimate=pl.CostEstimate(flops=20_000_000_000, bytes_accessed=30_000_000, transcendentals=0),

time: 57.5 us -> 59.3 us (1.031)
  Pallas kernels: 48 us -> 49.8 us
    pallas_call x1, Pallas kernels: 26.4 us -> 28.2 us  [local_step(): pl.pallas_call(functools.partial(rest_kernel, batch, heads, dim, tp), out...]
  transfers between devices with their start and end apart: 2 -> 2, of which waited for: 1 -> 1; matrix products, arithmetic and copies ran while one was open for 0% -> 0% of each run, Pallas kernels for 38% -> 37%
where the time goes in v3:
time: 59.3 us; the launch traced here: 59.1 us
  Pallas kernels  49.8 us (84%)
  waiting for transfers between devices  3.57 us (6%)
  starting transfers between devices  3.36 us (6%)
  local copies, waits for them, and re-layouts  1.07 us (2%)
  between operations  0.69 us (1%)
  other arithmetic  0.63 us (1%)
    pallas_call x1, Pallas kernels, local_step(): pl.pallas_call(functools.partial(rest_kernel, batch, heads, dim, tp), out...  28.2 us
    pallas_call x1, Pallas kernels, local_step(): pl.pallas_call(functools.partial(self_kernel, batch, heads, dim), out_sha...  21.6 us
    ppermute x1, waiting for transfers between devices, local_step(): wk_far = lax.ppermute(wk_c, 'tp', far)  3.57 us
    ppermute x1, starting transfers between devices, local_step(): wv_far = lax.ppermute(wv_cut, 'tp', far)  3.33 us
  transfers between devices with their start and end apart: 2, of which 1 were waited for; matrix products, arithmetic and copies ran while one was open for 0% of the time, Pallas kernels for 37%

profile of v3, /device:TPU:0, one launch (start us, length us, event | category | flops | bytes accessed | tf_op | source)
XLA Modules:
  0.0 59.1 jit_solution(3572987394072009184)
XLA Ops:
  0.6 1.1 %slice.3 = bf16[896,256]{1,0:T(8,128)(2,1)S(1)} slice(bf16[896,384]{1,0:T(8,128)(2,1)} %wv_h.3), slice={[0:896], [0:256]} | slice | bytes 917504 | tf_op jit(solution)/shard_map/slice | solution.py:410
  1.7 3.3 %collective-permute-start.1 = (bf16[896,256]{1,0:T(8,128)(2,1)S(1)}, bf16[896,256]{1,0:T(8,128)(2,1)S(1)}, u32[]{:S(2)}, u32[]{:S(2)}) collective-permute-start(bf16[896,256]{1,0:T(8,128)(2,1)S(1)} %slice.3), channel_id=1, source_target_pairs={{0,2},{1,3},{2,0},{3,1},{4,6},{5,7},{6,4},{7,5}} | collective-permute-start | bytes 1376264 | tf_op jit(solution)/shard_map/ppermute | solution.py:411
  5.0 0.0 collective-permute-start
  5.0 0.0 copy-start
  5.0 0.0 copy-start.1
  5.1 0.0 copy-start.2
  5.1 0.0 copy-start.3
  5.1 0.0 copy-start.4
  5.1 21.6 %self_attention.1 = (bf16[16,1536]{1,0:T(8,128)(2,1)S(1)}, bf16[3,16,128]{2,1,0:T(8,128)(2,1)}, bf16[3,16,128]{2,1,0:T(8,128)(2,1)}) custom-call(s32[16]{0:T(128)} %lens_h.1, bf16[16,1536]{1,0:T(8,128)(2,1)} %x_ref.1, f32[1536]{0:T(1024)} %g_h.1, f32[1536]{0:T(1024)} %b_h.1, bf16[16,3,4096,128]{3,2,1,0:T(8,128)(2,1)} %bitcast.5, ...), custom_call_target="tpu_custom_call" | custom-call | flops 40000000000 | bytes 60000000 | tf_op jit(solution)/shard_map/self_attention/pallas_call | solution.py:417
  26.7 0.0 collective-permute-done.1.wvr_h
  26.7 3.6 %collective-permute-done.wkr_h = bf16[896,384]{1,0:T(8,128)(2,1)S(1)} collective-permute-done((bf16[896,384]{1,0:T(8,128)(2,1)}, bf16[896,384]{1,0:T(8,128)(2,1)S(1)}, u32[]{:S(2)}, u32[]{:S(2)}) %collective-permute-start) | collective-permute-done | bytes 688160 | tf_op jit(solution)/shard_map/ppermute | solution.py:409
  30.3 0.0 copy-done
  30.3 0.0 copy-done.1
  30.3 0.0 copy-done.2
  30.3 0.0 copy-done.3
  30.3 0.0 copy-done.4
  30.3 28.2 %rest_of_layer.1 = f32[16,1536]{1,0:T(8,128)S(1)} custom-call(bf16[16,1536]{1,0:T(8,128)(2,1)S(1)} %get-tuple-element.6.part_ref, bf16[16,1536]{1,0:T(8,128)(2,1)S(1)} %copy-done, f32[1536]{0:T(1024)S(1)} %copy-done.1, f32[1536]{0:T(1024)S(1)} %copy-done.2, f32[1536]{0:T(1024)S(1)} %copy-done.3, f32[1536]{0:T(1024)S(1)} %copy-done.4, ...), custom_call_target="tpu_custom_call" | custom-call | flops 20000000000 | bytes 30000000 | tf_op jit(solution)/shard_map/rest_of_layer/pallas_call | solution.py:437
  58.5 0.6 %convert_element_type.3 = bf16[16,1536]{1,0:T(8,128)(2,1)} convert(f32[16,1536]{1,0:T(8,128)S(1)} %rest_of_layer.1) | non-fusion elementwise | flops 24576 | bytes 147456 | tf_op jit(solution)/shard_map/convert_element_type | solution.py:459
Async XLA Ops:
  1.7 25.0 %collective-permute-start.1 = (bf16[896,256]{1,0:T(8,128)(2,1)S(1)}, bf16[896,256]{1,0:T(8,128)(2,1)S(1)}, u32[]{:S(2)}, u32[]{:S(2)}) collective-permute-start(bf16[896,256]{1,0:T(8,128)(2,1)S(1)} %slice.3), channel_id=1, source_target_pairs={{0,2},{1,3},{2,0},{3,1},{4,6},{5,7},{6,4},{7,5}} | collective-permute-start | bytes 1376264 | tf_op jit(solution)/shard_map/ppermute | solution.py:411
  5.0 25.3 %collective-permute-start = (bf16[896,384]{1,0:T(8,128)(2,1)}, bf16[896,384]{1,0:T(8,128)(2,1)S(1)}, u32[]{:S(2)}, u32[]{:S(2)}) collective-permute-start(bf16[896,384]{1,0:T(8,128)(2,1)} %wk_h.3), channel_id=1, source_target_pairs={{0,2},{1,3},{2,0},{3,1},{4,6},{5,7},{6,4},{7,5}} | collective-permute-start | bytes 2064392 | tf_op jit(solution)/shard_map/ppermute | solution.py:409
  5.0 25.2 %copy-start = (bf16[16,1536]{1,0:T(8,128)(2,1)S(1)}, bf16[16,1536]{1,0:T(8,128)(2,1)}, u32[]{:S(2)}) copy-start(bf16[16,1536]{1,0:T(8,128)(2,1)} %x_ref.1) | copy-start | bytes 147460
  5.0 25.2 %copy-start.1 = (f32[1536]{0:T(1024)S(1)}, f32[1536]{0:T(1024)}, u32[]{:S(2)}) copy-start(f32[1536]{0:T(1024)} %g2.1) | copy-start | bytes 18436
  5.1 25.2 %copy-start.2 = (f32[1536]{0:T(1024)S(1)}, f32[1536]{0:T(1024)}, u32[]{:S(2)}) copy-start(f32[1536]{0:T(1024)} %b2.1) | copy-start | bytes 18436
  5.1 25.2 %copy-start.3 = (f32[1536]{0:T(1024)S(1)}, f32[1536]{0:T(1024)}, u32[]{:S(2)}) copy-start(f32[1536]{0:T(1024)} %g3.1) | copy-start | bytes 18436
  5.1 25.2 %copy-start.4 = (f32[1536]{0:T(1024)S(1)}, f32[1536]{0:T(1024)}, u32[]{:S(2)}) copy-start(f32[1536]{0:T(1024)} %b3.1) | copy-start | bytes 18436

commit v4 on v2

--- a/solution.py
+++ b/solution.py
@@ -198,7 +198,7 @@
 
 def rest_kernel(batch, heads, dim, tp, part_ref, x_ref, g2, b2, g3, b3, wqc_h, e_own_h, wk_h, wv_h, wkr_h, wvr_h, woc_h, wup_h, wdn_h,
                 out_ref,
-                wqc, enc, wkv, wkvr, woc, wup, wdn, kv_own, kv_rem, v_late, recv, send2, send3,
+                wqc, enc, wkv, wkvr, woc, wup, wdn, kv_own, kv_rem, v_late, far_in, both, near_in, send2, send3,
                 qc_s, qc_r, o_snd, o_rcv, o2_snd, o2_rcv, lsem, ssem, rsem, xs, xr, ns, nr):
     width = heads * dim
     scale = dim ** -0.5
@@ -232,24 +232,20 @@
         return pltpu.make_async_remote_copy(src_ref=src, dst_ref=dst, send_sem=send_sem, recv_sem=recv_sem,
                                             device_id={'tp': device}, device_id_type=pl.DeviceIdType.MESH)
 
-    def sum_copies(n, src):
-        return [remote(src, recv.at[n, me], ssem.at[n, d - 1], rsem.at[n, me], lax.rem(me + d, tp)) for d in range(1, tp)]
-
-    def exchange(n, src):
-        for copy in sum_copies(n, src):
-            copy.start()
-        recv[n, me] = src[...]
-
-    def collect(n, src):
-        for copy in sum_copies(n, src):
-            copy.wait_send()
-        for d in range(1, tp):
-            other = lax.rem(me + d, tp)
-            remote(src, recv.at[n, other], ssem.at[n, d - 1], rsem.at[n, other], other).wait_recv()
-        total = recv[n, 0].astype(F32)
-        for t in range(1, tp):
-            total = total + recv[n, t].astype(F32)
-        return total
+    def far_copy(n, src):
+        return remote(src, far_in.at[n], ssem.at[n, 0], rsem.at[n, 0], far)
+
+    def near_copy(n):
+        return remote(both.at[n], near_in.at[n], ssem.at[n, 1], rsem.at[n, 1], near)
+
+    def pass_on(n, src):
+        far_copy(n, src).wait()
+        both[n] = (src[...].astype(F32) + far_in[n].astype(F32)).astype(BF16)
+        near_copy(n).start()
+
+    def total(n):
+        near_copy(n).wait()
+        return both[n].astype(F32) + near_in[n].astype(F32)
 
     def project(first, count, jobs, tile=256):
         def body(i, c):
@@ -287,14 +283,17 @@
     own_job = (wkv, kv_own, 0, 2 * width)
     far_job = (wkvr, kv_rem, 0, width + early)
 
-    exchange(0, part_ref)
+    far_copy(0, part_ref).start()
     near_tokens(0).start()
     near_tokens(1).start()
     late(0).start()
     for copy in (ld_e0, ld_wk, ld_wv, ld_wkr, ld_wvr):
         copy.wait()
-    project(0, half, (own_job, far_job))
-    h1 = x_ref[...].astype(F32) + collect(0, part_ref)
+    before = half * 3 // 4
+    project(0, before, (own_job, far_job))
+    pass_on(0, part_ref)
+    project(before, half - before, (own_job, far_job))
+    h1 = x_ref[...].astype(F32) + total(0)
     c_norm = layer_norm(h1, g2[...].reshape(1, -1), b2[...].reshape(1, -1))
     ld_wqc.wait()
     qc_s[...] = dot(c_norm, wqc[...]).astype(BF16)
@@ -370,8 +369,9 @@
 
     def matmul_sum(n, lhs, weights, out):
         out[...] = dot(lhs, weights[...]).astype(BF16)
-        exchange(n, out)
-        return collect(n, out)
+        far_copy(n, out).start()
+        pass_on(n, out)
+        return total(n)
 
     ld_woc.wait()
     h2 = h1 + matmul_sum(1, oc, woc, send2)
@@ -428,11 +428,11 @@
             pltpu.VMEM((enc_dim, 2 * width), BF16), pltpu.VMEM((enc_dim, 2 * width), BF16),
             pltpu.VMEM((width, d_model), BF16), pltpu.VMEM((d_model, ff), BF16), pltpu.VMEM((ff, d_model), BF16),
             pltpu.VMEM((2 * n_enc, 2 * width), BF16), pltpu.VMEM((2 * n_enc, 2 * width), BF16), pltpu.VMEM((2 * n_enc, dim), F32),
-            pltpu.VMEM((3, tp, batch, d_model), BF16),
+            pltpu.VMEM((3, batch, d_model), BF16), pltpu.VMEM((3, batch, d_model), BF16), pltpu.VMEM((3, batch, d_model), BF16),
             pltpu.VMEM((batch, d_model), BF16), pltpu.VMEM((batch, d_model), BF16),
             pltpu.VMEM((batch, width), BF16), pltpu.VMEM((batch, width), BF16),
             pltpu.VMEM((heads * batch, dim), F32), pltpu.VMEM((heads * batch, dim), F32), pltpu.VMEM((batch, dim), F32), pltpu.VMEM((batch, dim), F32),
-            pltpu.SemaphoreType.DMA((9,)), pltpu.SemaphoreType.DMA((3, tp - 1)), pltpu.SemaphoreType.DMA((3, tp)),
+            pltpu.SemaphoreType.DMA((9,)), pltpu.SemaphoreType.DMA((3, 2)), pltpu.SemaphoreType.DMA((3, 2)),
             pltpu.SemaphoreType.DMA((5,)), pltpu.SemaphoreType.DMA((5,)), pltpu.SemaphoreType.DMA((2,)), pltpu.SemaphoreType.DMA((2,)),
         ],
         compiler_params=pltpu.CompilerParams(collective_id=0, has_side_effects=True, vmem_limit_bytes=46000000),

time: 57.5 us -> 58.5 us (1.017)
  Pallas kernels: 48 us -> 49 us
    pallas_call x1, Pallas kernels: 26.4 us -> 27.4 us  [local_step(): pl.pallas_call(functools.partial(rest_kernel, batch, heads, dim, tp), out...]
  transfers between devices with their start and end apart: 2 -> 2, of which waited for: 1 -> 1; matrix products, arithmetic and copies ran while one was open for 0% -> 0% of each run, Pallas kernels for 38% -> 37%
where the time goes in v4:
time: 58.5 us; the launch traced here: 58.4 us
  Pallas kernels  49 us (84%)
  waiting for transfers between devices  3.57 us (6%)
  starting transfers between devices  3.36 us (6%)
  local copies, waits for them, and re-layouts  1.07 us (2%)
  between operations  0.69 us (1%)
  other arithmetic  0.63 us (1%)
    pallas_call x1, Pallas kernels, local_step(): pl.pallas_call(functools.partial(rest_kernel, batch, heads, dim, tp), out...  27.4 us
    pallas_call x1, Pallas kernels, local_step(): pl.pallas_call(functools.partial(self_kernel, batch, heads, dim), out_sha...  21.6 us
    ppermute x1, waiting for transfers between devices, local_step(): wk_far = lax.ppermute(wk_c, 'tp', far)  3.57 us
    ppermute x1, starting transfers between devices, local_step(): wv_far = lax.ppermute(wv_cut, 'tp', far)  3.33 us
  transfers between devices with their start and end apart: 2, of which 1 were waited for; matrix products, arithmetic and copies ran while one was open for 0% of the time, Pallas kernels for 37%

profile of v4, /device:TPU:0, one launch (start us, length us, event | category | flops | bytes accessed | tf_op | source)
XLA Modules:
  0.0 58.4 jit_solution(3157629992982384890)
XLA Ops:
  0.6 1.1 %slice.3 = bf16[896,256]{1,0:T(8,128)(2,1)S(1)} slice(bf16[896,384]{1,0:T(8,128)(2,1)} %wv_h.3), slice={[0:896], [0:256]} | slice | bytes 917504 | tf_op jit(solution)/shard_map/slice | solution.py:394
  1.7 3.3 %collective-permute-start.1 = (bf16[896,256]{1,0:T(8,128)(2,1)S(1)}, bf16[896,256]{1,0:T(8,128)(2,1)S(1)}, u32[]{:S(2)}, u32[]{:S(2)}) collective-permute-start(bf16[896,256]{1,0:T(8,128)(2,1)S(1)} %slice.3), channel_id=1, source_target_pairs={{0,2},{1,3},{2,0},{3,1},{4,6},{5,7},{6,4},{7,5}} | collective-permute-start | bytes 1376264 | tf_op jit(solution)/shard_map/ppermute | solution.py:395
  5.0 0.0 collective-permute-start
  5.0 0.0 copy-start
  5.0 0.0 copy-start.1
  5.1 0.0 copy-start.2
  5.1 0.0 copy-start.3
  5.1 0.0 copy-start.4
  5.1 21.6 %self_attention.1 = (bf16[16,1536]{1,0:T(8,128)(2,1)S(1)}, bf16[3,16,128]{2,1,0:T(8,128)(2,1)}, bf16[3,16,128]{2,1,0:T(8,128)(2,1)}) custom-call(s32[16]{0:T(128)} %lens_h.1, bf16[16,1536]{1,0:T(8,128)(2,1)} %x_ref.1, f32[1536]{0:T(1024)} %g_h.1, f32[1536]{0:T(1024)} %b_h.1, bf16[16,3,4096,128]{3,2,1,0:T(8,128)(2,1)} %bitcast.5, ...), custom_call_target="tpu_custom_call" | custom-call | flops 40000000000 | bytes 60000000 | tf_op jit(solution)/shard_map/self_attention/pallas_call | solution.py:401
  26.7 0.0 collective-permute-done.1.wvr_h
  26.7 3.6 %collective-permute-done.wkr_h = bf16[896,384]{1,0:T(8,128)(2,1)S(1)} collective-permute-done((bf16[896,384]{1,0:T(8,128)(2,1)}, bf16[896,384]{1,0:T(8,128)(2,1)S(1)}, u32[]{:S(2)}, u32[]{:S(2)}) %collective-permute-start) | collective-permute-done | bytes 688160 | tf_op jit(solution)/shard_map/ppermute | solution.py:393
  30.3 0.0 copy-done
  30.3 0.0 copy-done.1
  30.3 0.0 copy-done.2
  30.3 0.0 copy-done.3
  30.3 0.0 copy-done.4
  30.3 27.4 %rest_of_layer.1 = f32[16,1536]{1,0:T(8,128)S(1)} custom-call(bf16[16,1536]{1,0:T(8,128)(2,1)S(1)} %get-tuple-element.6.part_ref, bf16[16,1536]{1,0:T(8,128)(2,1)S(1)} %copy-done, f32[1536]{0:T(1024)S(1)} %copy-done.1, f32[1536]{0:T(1024)S(1)} %copy-done.2, f32[1536]{0:T(1024)S(1)} %copy-done.3, f32[1536]{0:T(1024)S(1)} %copy-done.4, ...), custom_call_target="tpu_custom_call" | custom-call | flops 20000000000 | bytes 30000000 | tf_op jit(solution)/shard_map/rest_of_layer/pallas_call | solution.py:421
  57.7 0.6 %convert_element_type.3 = bf16[16,1536]{1,0:T(8,128)(2,1)} convert(f32[16,1536]{1,0:T(8,128)S(1)} %rest_of_layer.1) | non-fusion elementwise | flops 24576 | bytes 147456 | tf_op jit(solution)/shard_map/convert_element_type | solution.py:442
Async XLA Ops:
  1.7 25.0 %collective-permute-start.1 = (bf16[896,256]{1,0:T(8,128)(2,1)S(1)}, bf16[896,256]{1,0:T(8,128)(2,1)S(1)}, u32[]{:S(2)}, u32[]{:S(2)}) collective-permute-start(bf16[896,256]{1,0:T(8,128)(2,1)S(1)} %slice.3), channel_id=1, source_target_pairs={{0,2},{1,3},{2,0},{3,1},{4,6},{5,7},{6,4},{7,5}} | collective-permute-start | bytes 1376264 | tf_op jit(solution)/shard_map/ppermute | solution.py:395
  5.0 25.3 %collective-permute-start = (bf16[896,384]{1,0:T(8,128)(2,1)}, bf16[896,384]{1,0:T(8,128)(2,1)S(1)}, u32[]{:S(2)}, u32[]{:S(2)}) collective-permute-start(bf16[896,384]{1,0:T(8,128)(2,1)} %wk_h.3), channel_id=1, source_target_pairs={{0,2},{1,3},{2,0},{3,1},{4,6},{5,7},{6,4},{7,5}} | collective-permute-start | bytes 2064392 | tf_op jit(solution)/shard_map/ppermute | solution.py:393
  5.0 25.2 %copy-start = (bf16[16,1536]{1,0:T(8,128)(2,1)S(1)}, bf16[16,1536]{1,0:T(8,128)(2,1)}, u32[]{:S(2)}) copy-start(bf16[16,1536]{1,0:T(8,128)(2,1)} %x_ref.1) | copy-start | bytes 147460
  5.0 25.2 %copy-start.1 = (f32[1536]{0:T(1024)S(1)}, f32[1536]{0:T(1024)}, u32[]{:S(2)}) copy-start(f32[1536]{0:T(1024)} %g2.1) | copy-start | bytes 18436
  5.1 25.2 %copy-start.2 = (f32[1536]{0:T(1024)S(1)}, f32[1536]{0:T(1024)}, u32[]{:S(2)}) copy-start(f32[1536]{0:T(1024)} %b2.1) | copy-start | bytes 18436
  5.1 25.2 %copy-start.3 = (f32[1536]{0:T(1024)S(1)}, f32[1536]{0:T(1024)}, u32[]{:S(2)}) copy-start(f32[1536]{0:T(1024)} %g3.1) | copy-start | bytes 18436
  5.1 25.2 %copy-start.4 = (f32[1536]{0:T(1024)S(1)}, f32[1536]{0:T(1024)}, u32[]{:S(2)}) copy-start(f32[1536]{0:T(1024)} %b3.1) | copy-start | bytes 18436

commit v5 on v2

--- a/solution.py
+++ b/solution.py
@@ -213,9 +213,9 @@
         copy.start()
         return copy
 
+    ld_wv = load(2, wv_h, wkv.at[:, pl.ds(width, width)])
     ld_e0 = load(0, e_own_h, enc.at[pl.ds(0, half), :])
     ld_wk = load(1, wk_h, wkv.at[:, pl.ds(0, width)])
-    ld_wv = load(2, wv_h, wkv.at[:, pl.ds(width, width)])
     ld_wkr = load(3, wkr_h, wkvr.at[:, pl.ds(0, width)])
     ld_wvr = load(4, wvr_h, wkvr.at[:, pl.ds(width, early)])
     ld_wqc = load(5, wqc_h, wqc)
@@ -264,7 +264,7 @@
 
     def late(i):
         rows, cols = pl.ds(late_rows[i], late_rows[i + 1] - late_rows[i]), width - early
-        return remote(wv_h.at[rows, pl.ds(early, cols)], wkvr.at[rows, pl.ds(width + early, cols)], xs.at[3 + i], xr.at[3 + i], far)
+        return remote(wkv.at[rows, pl.ds(width + early, cols)], wkvr.at[rows, pl.ds(width + early, cols)], xs.at[3 + i], xr.at[3 + i], far)
 
     def late_product(i, tile=256):
         lo, hi = late_rows[i], late_rows[i + 1]
@@ -282,16 +282,18 @@
 
     def near_tokens(i):
         rows = half // 2
-        return remote(e_own_h.at[pl.ds(i * rows, rows), :], enc.at[pl.ds(half + i * rows, rows), :], ns.at[i], nr.at[i], near)
+        return remote(enc.at[pl.ds(i * rows, rows), :], enc.at[pl.ds(half + i * rows, rows), :], ns.at[i], nr.at[i], near)
 
     own_job = (wkv, kv_own, 0, 2 * width)
     far_job = (wkvr, kv_rem, 0, width + early)
 
     exchange(0, part_ref)
+    ld_wv.wait()
+    late(0).start()
+    ld_e0.wait()
     near_tokens(0).start()
     near_tokens(1).start()
-    late(0).start()
-    for copy in (ld_e0, ld_wk, ld_wv, ld_wkr, ld_wvr):
+    for copy in (ld_wk, ld_wkr, ld_wvr):
         copy.wait()
     project(0, half, (own_job, far_job))
     h1 = x_ref[...].astype(F32) + collect(0, part_ref)
@@ -304,8 +306,6 @@
     near_tokens(0).wait()
     near_tokens(1).wait()
     project(half, half, (far_job,))
-    late(0).wait()
-    late_product(0)
 
     rows = heads * batch
     row_b = lax.rem(lax.broadcasted_iota(jnp.int32, (rows, 128), 0), batch)
@@ -349,8 +349,9 @@
     o_snd[n_early * batch:(n_early + 1) * batch, :] = stats
     send_o = remote(o_snd, o_rcv, xs.at[1], xr.at[1], far)
     send_o.start()
-    late(1).wait()
-    late_product(1)
+    for i in range(2):
+        late(i).wait()
+        late_product(i)
     o2_snd[...] = mix(wide_r, kv_rem, n_early, heads)
     send_o2 = remote(o2_snd, o2_rcv, xs.at[2], xr.at[2], far)
     send_o2.start()

time: 57.5 us -> 58.3 us (1.014)
  Pallas kernels: 48 us -> 48.8 us
    pallas_call x1, Pallas kernels: 26.4 us -> 27.2 us  [local_step(): pl.pallas_call(functools.partial(rest_kernel, batch, heads, dim, tp), out...]
  transfers between devices with their start and end apart: 2 -> 2, of which waited for: 1 -> 1; matrix products, arithmetic and copies ran while one was open for 0% -> 0% of each run, Pallas kernels for 38% -> 37%
where the time goes in v5:
time: 58.3 us; the launch traced here: 58.1 us
  Pallas kernels  48.8 us (84%)
  waiting for transfers between devices  3.57 us (6%)
  starting transfers between devices  3.36 us (6%)
  local copies, waits for them, and re-layouts  1.07 us (2%)
  between operations  0.69 us (1%)
  other arithmetic  0.63 us (1%)
    pallas_call x1, Pallas kernels, local_step(): pl.pallas_call(functools.partial(rest_kernel, batch, heads, dim, tp), out...  27.2 us
    pallas_call x1, Pallas kernels, local_step(): pl.pallas_call(functools.partial(self_kernel, batch, heads, dim), out_sha...  21.6 us
    ppermute x1, waiting for transfers between devices, local_step(): wk_far = lax.ppermute(wk_c, 'tp', far)  3.57 us
    ppermute x1, starting transfers between devices, local_step(): wv_far = lax.ppermute(wv_cut, 'tp', far)  3.33 us
  transfers between devices with their start and end apart: 2, of which 1 were waited for; matrix products, arithmetic and copies ran while one was open for 0% of the time, Pallas kernels for 37%

profile of v5, /device:TPU:0, one launch (start us, length us, event | category | flops | bytes accessed | tf_op | source)
XLA Modules:
  0.0 58.1 jit_solution(16046074531617109256)
XLA Ops:
  0.6 1.1 %slice.3 = bf16[896,256]{1,0:T(8,128)(2,1)S(1)} slice(bf16[896,384]{1,0:T(8,128)(2,1)} %wv_h.3), slice={[0:896], [0:256]} | slice | bytes 917504 | tf_op jit(solution)/shard_map/slice | solution.py:395
  1.7 3.3 %collective-permute-start.1 = (bf16[896,256]{1,0:T(8,128)(2,1)S(1)}, bf16[896,256]{1,0:T(8,128)(2,1)S(1)}, u32[]{:S(2)}, u32[]{:S(2)}) collective-permute-start(bf16[896,256]{1,0:T(8,128)(2,1)S(1)} %slice.3), channel_id=1, source_target_pairs={{0,2},{1,3},{2,0},{3,1},{4,6},{5,7},{6,4},{7,5}} | collective-permute-start | bytes 1376264 | tf_op jit(solution)/shard_map/ppermute | solution.py:396
  5.0 0.0 collective-permute-start
  5.0 0.0 copy-start
  5.0 0.0 copy-start.1
  5.1 0.0 copy-start.2
  5.1 0.0 copy-start.3
  5.1 0.0 copy-start.4
  5.1 21.6 %self_attention.1 = (bf16[16,1536]{1,0:T(8,128)(2,1)S(1)}, bf16[3,16,128]{2,1,0:T(8,128)(2,1)}, bf16[3,16,128]{2,1,0:T(8,128)(2,1)}) custom-call(s32[16]{0:T(128)} %lens_h.1, bf16[16,1536]{1,0:T(8,128)(2,1)} %x_ref.1, f32[1536]{0:T(1024)} %g_h.1, f32[1536]{0:T(1024)} %b_h.1, bf16[16,3,4096,128]{3,2,1,0:T(8,128)(2,1)} %bitcast.5, ...), custom_call_target="tpu_custom_call" | custom-call | flops 40000000000 | bytes 60000000 | tf_op jit(solution)/shard_map/self_attention/pallas_call | solution.py:402
  26.7 0.0 collective-permute-done.1.wvr_h
  26.7 3.6 %collective-permute-done.wkr_h = bf16[896,384]{1,0:T(8,128)(2,1)S(1)} collective-permute-done((bf16[896,384]{1,0:T(8,128)(2,1)}, bf16[896,384]{1,0:T(8,128)(2,1)S(1)}, u32[]{:S(2)}, u32[]{:S(2)}) %collective-permute-start) | collective-permute-done | bytes 688160 | tf_op jit(solution)/shard_map/ppermute | solution.py:394
  30.3 0.0 copy-done
  30.3 0.0 copy-done.1
  30.3 0.0 copy-done.2
  30.3 0.0 copy-done.3
  30.3 0.0 copy-done.4
  30.3 27.2 %rest_of_layer.1 = f32[16,1536]{1,0:T(8,128)S(1)} custom-call(bf16[16,1536]{1,0:T(8,128)(2,1)S(1)} %get-tuple-element.6.part_ref, bf16[16,1536]{1,0:T(8,128)(2,1)S(1)} %copy-done, f32[1536]{0:T(1024)S(1)} %copy-done.1, f32[1536]{0:T(1024)S(1)} %copy-done.2, f32[1536]{0:T(1024)S(1)} %copy-done.3, f32[1536]{0:T(1024)S(1)} %copy-done.4, ...), custom_call_target="tpu_custom_call" | custom-call | flops 20000000000 | bytes 30000000 | tf_op jit(solution)/shard_map/rest_of_layer/pallas_call | solution.py:422
  57.5 0.6 %convert_element_type.3 = bf16[16,1536]{1,0:T(8,128)(2,1)} convert(f32[16,1536]{1,0:T(8,128)S(1)} %rest_of_layer.1) | non-fusion elementwise | flops 24576 | bytes 147456 | tf_op jit(solution)/shard_map/convert_element_type | solution.py:443
Async XLA Ops:
  1.7 25.0 %collective-permute-start.1 = (bf16[896,256]{1,0:T(8,128)(2,1)S(1)}, bf16[896,256]{1,0:T(8,128)(2,1)S(1)}, u32[]{:S(2)}, u32[]{:S(2)}) collective-permute-start(bf16[896,256]{1,0:T(8,128)(2,1)S(1)} %slice.3), channel_id=1, source_target_pairs={{0,2},{1,3},{2,0},{3,1},{4,6},{5,7},{6,4},{7,5}} | collective-permute-start | bytes 1376264 | tf_op jit(solution)/shard_map/ppermute | solution.py:396
  5.0 25.3 %collective-permute-start = (bf16[896,384]{1,0:T(8,128)(2,1)}, bf16[896,384]{1,0:T(8,128)(2,1)S(1)}, u32[]{:S(2)}, u32[]{:S(2)}) collective-permute-start(bf16[896,384]{1,0:T(8,128)(2,1)} %wk_h.3), channel_id=1, source_target_pairs={{0,2},{1,3},{2,0},{3,1},{4,6},{5,7},{6,4},{7,5}} | collective-permute-start | bytes 2064392 | tf_op jit(solution)/shard_map/ppermute | solution.py:394
  5.0 25.2 %copy-start = (bf16[16,1536]{1,0:T(8,128)(2,1)S(1)}, bf16[16,1536]{1,0:T(8,128)(2,1)}, u32[]{:S(2)}) copy-start(bf16[16,1536]{1,0:T(8,128)(2,1)} %x_ref.1) | copy-start | bytes 147460
  5.0 25.2 %copy-start.1 = (f32[1536]{0:T(1024)S(1)}, f32[1536]{0:T(1024)}, u32[]{:S(2)}) copy-start(f32[1536]{0:T(1024)} %g2.1) | copy-start | bytes 18436
  5.1 25.2 %copy-start.2 = (f32[1536]{0:T(1024)S(1)}, f32[1536]{0:T(1024)}, u32[]{:S(2)}) copy-start(f32[1536]{0:T(1024)} %b2.1) | copy-start | bytes 18436
  5.1 25.2 %copy-start.3 = (f32[1536]{0:T(1024)S(1)}, f32[1536]{0:T(1024)}, u32[]{:S(2)}) copy-start(f32[1536]{0:T(1024)} %g3.1) | copy-start | bytes 18436
  5.1 25.2 %copy-start.4 = (f32[1536]{0:T(1024)S(1)}, f32[1536]{0:T(1024)}, u32[]{:S(2)}) copy-start(f32[1536]{0:T(1024)} %b3.1) | copy-start | bytes 18436

commit v6 on v5

--- a/solution.py
+++ b/solution.py
@@ -16,6 +16,7 @@
 UNROLL = 4
 GRAIN = 64
 GROUPS = 6
+ENC_STEPS = 4
 
 
 def layer_norm(values, ln_gain, ln_bias):
@@ -37,9 +38,9 @@
     return [pltpu.with_memory_space_constraint(a, pltpu.HBM) for a in arrays]
 
 
-def self_kernel(batch, heads, dim, lens_h, x_h, g_h, b_h, kc, vc, wq_h, wk_h, wv_h, wo_h,
-                part_ref, knew_ref, vnew_ref,
-                lens, x_v, g_v, b_v, wq, wk, wv, wo, kbuf, vbuf, q_s, v_s, o_s, m_s, l_s, acc_s, new_s, wsem, ksem, vsem):
+def self_kernel(batch, heads, dim, lens_h, x_h, g_h, b_h, kc, vc, wq_h, wk_h, wv_h, wo_h, e_h, wkc_h, wvc_h,
+                part_ref, knew_ref, vnew_ref, kv_ref,
+                lens, x_v, g_v, b_v, wq, wk, wv, wo, kbuf, vbuf, q_s, v_s, o_s, m_s, l_s, acc_s, new_s, enc, wkv, wsem, ksem, vsem, esem):
     width = heads * dim
     scale = dim ** -0.5
     pairs = ((x_h, x_v), (g_h, g_v), (b_h, b_v), (wq_h, wq), (lens_h, lens), (wk_h, wk), (wv_h, wv), (wo_h, wo))
@@ -79,6 +80,11 @@
     for group in range(GROUPS):
         ptr = fetch_group(group, ptr, True)
     ld_o.start()
+    enc_loads = [pltpu.make_async_copy(src, dst, esem.at[i]) for i, (src, dst) in enumerate(
+        ((e_h, enc), (wkc_h, wkv.at[:, pl.ds(0, width)]), (wvc_h, wkv.at[:, pl.ds(width, width)])))]
+    for copy in enc_loads:
+        copy.start()
+    enc_tile = enc.shape[0] // ENC_STEPS
 
     n_items = jnp.int32(0)
     for seq in range(batch):
@@ -128,6 +134,13 @@
         @pl.when(i == 1)
         def _():
             new_token()
+            for copy in enc_loads:
+                copy.wait()
+
+        @pl.when((i >= 1) & (i <= ENC_STEPS))
+        def _():
+            rows = pl.ds(pl.multiple_of((i - 1) * enc_tile, enc_tile), enc_tile)
+            kv_ref[rows, :] = dot(enc[rows, :], wkv[...]).astype(BF16)
 
         items = []
         for u in range(UNROLL):
@@ -196,7 +209,7 @@
     part_ref[...] = dot(o_s[...].astype(BF16), wo[...]).astype(BF16)
 
 
-def rest_kernel(batch, heads, dim, tp, part_ref, x_ref, g2, b2, g3, b3, wqc_h, e_own_h, wk_h, wv_h, wkr_h, wvr_h, woc_h, wup_h, wdn_h,
+def rest_kernel(batch, heads, dim, tp, part_ref, x_ref, g2, b2, g3, b3, wqc_h, e_own_h, wk_h, wv_h, wkr_h, wvr_h, kv_h, woc_h, wup_h, wdn_h,
                 out_ref,
                 wqc, enc, wkv, wkvr, woc, wup, wdn, kv_own, kv_rem, v_late, recv, send2, send3,
                 qc_s, qc_r, o_snd, o_rcv, o2_snd, o2_rcv, lsem, ssem, rsem, xs, xr, ns, nr):
@@ -222,6 +235,7 @@
     ld_woc = load(6, woc_h, woc)
     ld_up = load(7, wup_h, wup)
     ld_dn = load(8, wdn_h, wdn)
+    ld_kv = load(9, kv_h, kv_own.at[pl.ds(0, half), :])
 
     barrier = pltpu.get_barrier_semaphore()
     for d in range(1, tp):
@@ -293,9 +307,11 @@
     ld_e0.wait()
     near_tokens(0).start()
     near_tokens(1).start()
-    for copy in (ld_wk, ld_wkr, ld_wvr):
+    for copy in (ld_wkr, ld_wvr):
         copy.wait()
-    project(0, half, (own_job, far_job))
+    project(0, half, (far_job,))
+    near_tokens(0).wait()
+    project(half, half // 2, (far_job,))
     h1 = x_ref[...].astype(F32) + collect(0, part_ref)
     c_norm = layer_norm(h1, g2[...].reshape(1, -1), b2[...].reshape(1, -1))
     ld_wqc.wait()
@@ -303,9 +319,10 @@
     send_q = remote(qc_s, qc_r, xs.at[0], xr.at[0], far)
     send_q.start()
     late(1).start()
-    near_tokens(0).wait()
     near_tokens(1).wait()
-    project(half, half, (far_job,))
+    project(half + half // 2, half // 2, (far_job,))
+    late(0).wait()
+    late_product(0)
 
     rows = heads * batch
     row_b = lax.rem(lax.broadcasted_iota(jnp.int32, (rows, 128), 0), batch)
@@ -349,13 +366,14 @@
     o_snd[n_early * batch:(n_early + 1) * batch, :] = stats
     send_o = remote(o_snd, o_rcv, xs.at[1], xr.at[1], far)
     send_o.start()
-    for i in range(2):
-        late(i).wait()
-        late_product(i)
+    late(1).wait()
+    late_product(1)
     o2_snd[...] = mix(wide_r, kv_rem, n_early, heads)
     send_o2 = remote(o2_snd, o2_rcv, xs.at[2], xr.at[2], far)
     send_o2.start()
+    ld_wk.wait()
     project(half, half, (own_job,))
+    ld_kv.wait()
     m_a, l_a, wide_a = weigh(qc_s[...], kv_own)
     o_a = mix(wide_a, kv_own, 0, heads)
     send_o.wait()
@@ -399,30 +417,32 @@
     hbm = pl.BlockSpec(memory_space=pltpu.HBM)
     vmem = pl.BlockSpec(memory_space=pltpu.VMEM)
     slots = GROUPS * UNROLL
-    part, k_new, v_new = pl.pallas_call(
+    part, k_new, v_new, kv_half = pl.pallas_call(
         functools.partial(self_kernel, batch, heads, dim),
-        out_shape=(jax.ShapeDtypeStruct((batch, d_model), BF16), jax.ShapeDtypeStruct((heads, batch, dim), BF16), jax.ShapeDtypeStruct((heads, batch, dim), BF16)),
-        in_specs=[hbm] * 10,
-        out_specs=(vmem, vmem, vmem),
+        out_shape=(jax.ShapeDtypeStruct((batch, d_model), BF16), jax.ShapeDtypeStruct((heads, batch, dim), BF16), jax.ShapeDtypeStruct((heads, batch, dim), BF16),
+                   jax.ShapeDtypeStruct((enc.shape[0], 2 * width), BF16)),
+        in_specs=[hbm] * 13,
+        out_specs=(vmem, vmem, vmem, vmem),
         scratch_shapes=[
             pltpu.SMEM((batch,), jnp.int32), pltpu.VMEM((batch, d_model), BF16), pltpu.VMEM((d_model,), F32), pltpu.VMEM((d_model,), F32),
             pltpu.VMEM((d_model, width), BF16), pltpu.VMEM((d_model, width), BF16), pltpu.VMEM((d_model, width), BF16), pltpu.VMEM((width, d_model), BF16),
             pltpu.VMEM((slots, heads, CHUNK, dim), BF16), pltpu.VMEM((slots, heads, CHUNK, dim), BF16),
             pltpu.VMEM((batch + 8, width), F32), pltpu.VMEM((batch, width), F32), pltpu.VMEM((batch, width), F32),
             pltpu.VMEM((batch + 1, 8, dim), F32), pltpu.VMEM((batch + 1, 8, dim), F32), pltpu.VMEM((batch + 1, 8, 2 * dim), F32), pltpu.VMEM((batch, 8, dim), F32),
-            pltpu.SemaphoreType.DMA((8,)), pltpu.SemaphoreType.DMA((slots,)), pltpu.SemaphoreType.DMA((slots,)),
+            pltpu.VMEM(enc.shape, BF16), pltpu.VMEM((enc.shape[1], 2 * width), BF16),
+            pltpu.SemaphoreType.DMA((8,)), pltpu.SemaphoreType.DMA((slots,)), pltpu.SemaphoreType.DMA((slots,)), pltpu.SemaphoreType.DMA((3,)),
         ],
         compiler_params=pltpu.CompilerParams(vmem_limit_bytes=46000000),
         cost_estimate=pl.CostEstimate(flops=40_000_000_000, bytes_accessed=60_000_000, transcendentals=0),
         name='self_attention',
-    )(*in_hbm(seq_lens, x, ln1_gain, ln1_bias, jnp.transpose(k_cache, (0, 2, 1, 3)), jnp.transpose(v_cache, (0, 2, 1, 3)), w_q, w_k, w_v, w_o))
+    )(*in_hbm(seq_lens, x, ln1_gain, ln1_bias, jnp.transpose(k_cache, (0, 2, 1, 3)), jnp.transpose(v_cache, (0, 2, 1, 3)), w_q, w_k, w_v, w_o, enc, wk_c, wv_c))
 
     n_enc, enc_dim = enc.shape
     ff = w_up.shape[1]
     out = pl.pallas_call(
         functools.partial(rest_kernel, batch, heads, dim, tp),
         out_shape=jax.ShapeDtypeStruct((batch, d_model), F32),
-        in_specs=[vmem] * 6 + [hbm] * 4 + [any_spec] * 2 + [hbm] * 3,
+        in_specs=[vmem] * 6 + [hbm] * 4 + [any_spec] * 3 + [hbm] * 3,
         out_specs=vmem,
         scratch_shapes=[
             pltpu.VMEM((d_model, width), BF16), pltpu.VMEM((2 * n_enc, enc_dim), BF16),
@@ -433,13 +453,13 @@
             pltpu.VMEM((batch, d_model), BF16), pltpu.VMEM((batch, d_model), BF16),
             pltpu.VMEM((batch, width), BF16), pltpu.VMEM((batch, width), BF16),
             pltpu.VMEM((heads * batch, dim), F32), pltpu.VMEM((heads * batch, dim), F32), pltpu.VMEM((batch, dim), F32), pltpu.VMEM((batch, dim), F32),
-            pltpu.SemaphoreType.DMA((9,)), pltpu.SemaphoreType.DMA((3, tp - 1)), pltpu.SemaphoreType.DMA((3, tp)),
+            pltpu.SemaphoreType.DMA((10,)), pltpu.SemaphoreType.DMA((3, tp - 1)), pltpu.SemaphoreType.DMA((3, tp)),
             pltpu.SemaphoreType.DMA((5,)), pltpu.SemaphoreType.DMA((5,)), pltpu.SemaphoreType.DMA((2,)), pltpu.SemaphoreType.DMA((2,)),
         ],
         compiler_params=pltpu.CompilerParams(collective_id=0, has_side_effects=True, vmem_limit_bytes=46000000),
         cost_estimate=pl.CostEstimate(flops=20_000_000_000, bytes_accessed=30_000_000, transcendentals=0),
         name='rest_of_layer',
-    )(part, x, ln2_gain, ln2_bias, ln3_gain, ln3_bias, *in_hbm(wq_c, enc, wk_c, wv_c), wk_far, wv_far, *in_hbm(wo_c, w_up, w_down))
+    )(part, x, ln2_gain, ln2_bias, ln3_gain, ln3_bias, *in_hbm(wq_c, enc, wk_c, wv_c), wk_far, wv_far, kv_half, *in_hbm(wo_c, w_up, w_down))
     return out.astype(BF16), jnp.transpose(k_new, (1, 0, 2)), jnp.transpose(v_new, (1, 0, 2))
 
 

time: 58.3 us -> 59.7 us (1.024)
  Pallas kernels: 48.8 us -> 53.8 us
  waiting for transfers between devices: 3.57 us -> 0.01 us
    pallas_call x1, Pallas kernels: 21.6 us -> 27.3 us  [local_step(): pl.pallas_call(functools.partial(self_kernel, batch, heads, dim), out_sha...]
    ppermute x1, waiting for transfers between devices: 3.57 us -> 0.01 us  [local_step(): wk_far = lax.ppermute(wk_c, 'tp', far)]
    pallas_call x1, Pallas kernels: 27.2 us -> 26.4 us  [local_step(): pl.pallas_call(functools.partial(rest_kernel, batch, heads, dim, tp), out...]
  transfers between devices with their start and end apart: 2 -> 2, of which waited for: 1 -> 0; matrix products, arithmetic and copies ran while one was open for 0% -> 0% of each run, Pallas kernels for 37% -> 46%
where the time goes in v6:
time: 59.7 us; the launch traced here: 59.6 us
  Pallas kernels  53.8 us (90%)
  starting transfers between devices  3.36 us (6%)
  local copies, waits for them, and re-layouts  1.07 us (2%)
  between operations  0.72 us (1%)
  other arithmetic  0.63 us (1%)
    pallas_call x1, Pallas kernels, local_step(): pl.pallas_call(functools.partial(self_kernel, batch, heads, dim), out_sha...  27.3 us
    pallas_call x1, Pallas kernels, local_step(): pl.pallas_call(functools.partial(rest_kernel, batch, heads, dim, tp), out...  26.4 us
    ppermute x1, starting transfers between devices, local_step(): wv_far = lax.ppermute(wv_cut, 'tp', far)  3.33 us
  transfers between devices with their start and end apart: 2, of which 0 were waited for; matrix products, arithmetic and copies ran while one was open for 0% of the time, Pallas kernels for 46%

profile of v6, /device:TPU:0, one launch (start us, length us, event | category | flops | bytes accessed | tf_op | source)
XLA Modules:
  0.0 59.6 jit_solution(787817381070813119)
XLA Ops:
  0.6 1.1 %slice.3 = bf16[896,256]{1,0:T(8,128)(2,1)S(1)} slice(bf16[896,384]{1,0:T(8,128)(2,1)} %wv_h.3), slice={[0:896], [0:256]} | slice | bytes 917504 | tf_op jit(solution)/shard_map/slice | solution.py:413
  1.7 3.3 %collective-permute-start.1 = (bf16[896,256]{1,0:T(8,128)(2,1)S(1)}, bf16[896,256]{1,0:T(8,128)(2,1)S(1)}, u32[]{:S(2)}, u32[]{:S(2)}) collective-permute-start(bf16[896,256]{1,0:T(8,128)(2,1)S(1)} %slice.3), channel_id=1, source_target_pairs={{0,2},{1,3},{2,0},{3,1},{4,6},{5,7},{6,4},{7,5}} | collective-permute-start | bytes 1376264 | tf_op jit(solution)/shard_map/ppermute | solution.py:414
  5.0 0.0 collective-permute-start
  5.0 0.0 copy-start
  5.0 0.0 copy-start.1
  5.1 0.0 copy-start.2
  5.1 0.0 copy-start.3
  5.1 0.0 copy-start.4
  5.1 27.3 %self_attention.1 = (bf16[16,1536]{1,0:T(8,128)(2,1)S(1)}, bf16[3,16,128]{2,1,0:T(8,128)(2,1)}, bf16[3,16,128]{2,1,0:T(8,128)(2,1)}, bf16[1024,768]{1,0:T(8,128)(2,1)S(1)}) custom-call(s32[16]{0:T(128)} %lens_h.1, bf16[16,1536]{1,0:T(8,128)(2,1)} %x_ref.1, f32[1536]{0:T(1024)} %g_h.1, f32[1536]{0:T(1024)} %b_h.1, bf16[16,3,4096,128]{3,2,1,0:T(8,128)(2,1)} %bitcast.5, ...), custom_call_target="tpu_custom_call" | custom-call | flops 40000000000 | bytes 60000000 | tf_op jit(solution)/shard_map/self_attention/pallas_call | solution.py:420
  32.4 0.0 collective-permute-done.1.wvr_h
  32.4 0.0 collective-permute-done.wkr_h
  32.4 0.0 copy-done
  32.5 0.0 copy-done.1
  32.5 0.0 copy-done.2
  32.5 0.0 copy-done.3
  32.5 0.0 copy-done.4
  32.5 26.4 %rest_of_layer.1 = f32[16,1536]{1,0:T(8,128)S(1)} custom-call(bf16[16,1536]{1,0:T(8,128)(2,1)S(1)} %get-tuple-element.7.part_ref, bf16[16,1536]{1,0:T(8,128)(2,1)S(1)} %copy-done, f32[1536]{0:T(1024)S(1)} %copy-done.1, f32[1536]{0:T(1024)S(1)} %copy-done.2, f32[1536]{0:T(1024)S(1)} %copy-done.3, f32[1536]{0:T(1024)S(1)} %copy-done.4, ...), custom_call_target="tpu_custom_call" | custom-call | flops 20000000000 | bytes 30000000 | tf_op jit(solution)/shard_map/rest_of_layer/pallas_call | solution.py:442
  58.9 0.6 %convert_element_type.3 = bf16[16,1536]{1,0:T(8,128)(2,1)} convert(f32[16,1536]{1,0:T(8,128)S(1)} %rest_of_layer.1) | non-fusion elementwise | flops 24576 | bytes 147456 | tf_op jit(solution)/shard_map/convert_element_type | solution.py:463
Async XLA Ops:
  1.7 30.7 %collective-permute-start.1 = (bf16[896,256]{1,0:T(8,128)(2,1)S(1)}, bf16[896,256]{1,0:T(8,128)(2,1)S(1)}, u32[]{:S(2)}, u32[]{:S(2)}) collective-permute-start(bf16[896,256]{1,0:T(8,128)(2,1)S(1)} %slice.3), channel_id=1, source_target_pairs={{0,2},{1,3},{2,0},{3,1},{4,6},{5,7},{6,4},{7,5}} | collective-permute-start | bytes 1376264 | tf_op jit(solution)/shard_map/ppermute | solution.py:414
  5.0 27.4 %collective-permute-start = (bf16[896,384]{1,0:T(8,128)(2,1)}, bf16[896,384]{1,0:T(8,128)(2,1)S(1)}, u32[]{:S(2)}, u32[]{:S(2)}) collective-permute-start(bf16[896,384]{1,0:T(8,128)(2,1)} %wk_h.3), channel_id=1, source_target_pairs={{0,2},{1,3},{2,0},{3,1},{4,6},{5,7},{6,4},{7,5}} | collective-permute-start | bytes 2064392 | tf_op jit(solution)/shard_map/ppermute | solution.py:412
  5.0 27.4 %copy-start = (bf16[16,1536]{1,0:T(8,128)(2,1)S(1)}, bf16[16,1536]{1,0:T(8,128)(2,1)}, u32[]{:S(2)}) copy-start(bf16[16,1536]{1,0:T(8,128)(2,1)} %x_ref.1) | copy-start | bytes 147460
  5.0 27.4 %copy-start.1 = (f32[1536]{0:T(1024)S(1)}, f32[1536]{0:T(1024)}, u32[]{:S(2)}) copy-start(f32[1536]{0:T(1024)} %g2.1) | copy-start | bytes 18436
  5.1 27.4 %copy-start.2 = (f32[1536]{0:T(1024)S(1)}, f32[1536]{0:T(1024)}, u32[]{:S(2)}) copy-start(f32[1536]{0:T(1024)} %b2.1) | copy-start | bytes 18436
  5.1 27.4 %copy-start.3 = (f32[1536]{0:T(1024)S(1)}, f32[1536]{0:T(1024)}, u32[]{:S(2)}) copy-start(f32[1536]{0:T(1024)} %g3.1) | copy-start | bytes 18436
  5.1 27.4 %copy-start.4 = (f32[1536]{0:T(1024)S(1)}, f32[1536]{0:T(1024)}, u32[]{:S(2)}) copy-start(f32[1536]{0:T(1024)} %b3.1) | copy-start | bytes 18436

commit v7 on v5

--- a/solution.py
+++ b/solution.py
@@ -260,7 +260,7 @@
 
         lax.fori_loop(first // tile, (first + count) // tile, body, 0)
 
-    late_rows = (0, 512, wv_h.shape[0])
+    late_rows = (0, 640, wv_h.shape[0])
 
     def late(i):
         rows, cols = pl.ds(late_rows[i], late_rows[i + 1] - late_rows[i]), width - early
@@ -306,6 +306,8 @@
     near_tokens(0).wait()
     near_tokens(1).wait()
     project(half, half, (far_job,))
+    late(0).wait()
+    late_product(0)
 
     rows = heads * batch
     row_b = lax.rem(lax.broadcasted_iota(jnp.int32, (rows, 128), 0), batch)
@@ -349,9 +351,8 @@
     o_snd[n_early * batch:(n_early + 1) * batch, :] = stats
     send_o = remote(o_snd, o_rcv, xs.at[1], xr.at[1], far)
     send_o.start()
-    for i in range(2):
-        late(i).wait()
-        late_product(i)
+    late(1).wait()
+    late_product(1)
     o2_snd[...] = mix(wide_r, kv_rem, n_early, heads)
     send_o2 = remote(o2_snd, o2_rcv, xs.at[2], xr.at[2], far)
     send_o2.start()

time: 58.3 us -> 57.7 us (0.990)
  transfers between devices with their start and end apart: 2 -> 2, of which waited for: 1 -> 1; matrix products, arithmetic and copies ran while one was open for 0% -> 0% of each run, Pallas kernels for 37% -> 38%
where the time goes in v7:
time: 57.7 us; the launch traced here: 57.6 us
  Pallas kernels  48.3 us (84%)
  waiting for transfers between devices  3.57 us (6%)
  starting transfers between devices  3.36 us (6%)
  local copies, waits for them, and re-layouts  1.07 us (2%)
  between operations  0.69 us (1%)
  other arithmetic  0.63 us (1%)
    pallas_call x1, Pallas kernels, local_step(): pl.pallas_call(functools.partial(rest_kernel, batch, heads, dim, tp), out...  26.7 us
    pallas_call x1, Pallas kernels, local_step(): pl.pallas_call(functools.partial(self_kernel, batch, heads, dim), out_sha...  21.6 us
    ppermute x1, waiting for transfers between devices, local_step(): wk_far = lax.ppermute(wk_c, 'tp', far)  3.57 us
    ppermute x1, starting transfers between devices, local_step(): wv_far = lax.ppermute(wv_cut, 'tp', far)  3.33 us
  transfers between devices with their start and end apart: 2, of which 1 were waited for; matrix products, arithmetic and copies ran while one was open for 0% of the time, Pallas kernels for 38%

profile of v7, /device:TPU:0, one launch (start us, length us, event | category | flops | bytes accessed | tf_op | source)
XLA Modules:
  0.0 57.6 jit_solution(14591466397623189581)
XLA Ops:
  0.6 1.1 %slice.3 = bf16[896,256]{1,0:T(8,128)(2,1)S(1)} slice(bf16[896,384]{1,0:T(8,128)(2,1)} %wv_h.3), slice={[0:896], [0:256]} | slice | bytes 917504 | tf_op jit(solution)/shard_map/slice | solution.py:396
  1.7 3.3 %collective-permute-start.1 = (bf16[896,256]{1,0:T(8,128)(2,1)S(1)}, bf16[896,256]{1,0:T(8,128)(2,1)S(1)}, u32[]{:S(2)}, u32[]{:S(2)}) collective-permute-start(bf16[896,256]{1,0:T(8,128)(2,1)S(1)} %slice.3), channel_id=1, source_target_pairs={{0,2},{1,3},{2,0},{3,1},{4,6},{5,7},{6,4},{7,5}} | collective-permute-start | bytes 1376264 | tf_op jit(solution)/shard_map/ppermute | solution.py:397
  5.0 0.0 collective-permute-start
  5.0 0.0 copy-start
  5.0 0.0 copy-start.1
  5.1 0.0 copy-start.2
  5.1 0.0 copy-start.3
  5.1 0.0 copy-start.4
  5.1 21.6 %self_attention.1 = (bf16[16,1536]{1,0:T(8,128)(2,1)S(1)}, bf16[3,16,128]{2,1,0:T(8,128)(2,1)}, bf16[3,16,128]{2,1,0:T(8,128)(2,1)}) custom-call(s32[16]{0:T(128)} %lens_h.1, bf16[16,1536]{1,0:T(8,128)(2,1)} %x_ref.1, f32[1536]{0:T(1024)} %g_h.1, f32[1536]{0:T(1024)} %b_h.1, bf16[16,3,4096,128]{3,2,1,0:T(8,128)(2,1)} %bitcast.5, ...), custom_call_target="tpu_custom_call" | custom-call | flops 40000000000 | bytes 60000000 | tf_op jit(solution)/shard_map/self_attention/pallas_call | solution.py:403
  26.7 0.0 collective-permute-done.1.wvr_h
  26.7 3.6 %collective-permute-done.wkr_h = bf16[896,384]{1,0:T(8,128)(2,1)S(1)} collective-permute-done((bf16[896,384]{1,0:T(8,128)(2,1)}, bf16[896,384]{1,0:T(8,128)(2,1)S(1)}, u32[]{:S(2)}, u32[]{:S(2)}) %collective-permute-start) | collective-permute-done | bytes 688160 | tf_op jit(solution)/shard_map/ppermute | solution.py:395
  30.3 0.0 copy-done
  30.3 0.0 copy-done.1
  30.3 0.0 copy-done.2
  30.3 0.0 copy-done.3
  30.3 0.0 copy-done.4
  30.3 26.7 %rest_of_layer.1 = f32[16,1536]{1,0:T(8,128)S(1)} custom-call(bf16[16,1536]{1,0:T(8,128)(2,1)S(1)} %get-tuple-element.6.part_ref, bf16[16,1536]{1,0:T(8,128)(2,1)S(1)} %copy-done, f32[1536]{0:T(1024)S(1)} %copy-done.1, f32[1536]{0:T(1024)S(1)} %copy-done.2, f32[1536]{0:T(1024)S(1)} %copy-done.3, f32[1536]{0:T(1024)S(1)} %copy-done.4, ...), custom_call_target="tpu_custom_call" | custom-call | flops 20000000000 | bytes 30000000 | tf_op jit(solution)/shard_map/rest_of_layer/pallas_call | solution.py:423
  57.0 0.6 %convert_element_type.3 = bf16[16,1536]{1,0:T(8,128)(2,1)} convert(f32[16,1536]{1,0:T(8,128)S(1)} %rest_of_layer.1) | non-fusion elementwise | flops 24576 | bytes 147456 | tf_op jit(solution)/shard_map/convert_element_type | solution.py:444
Async XLA Ops:
  1.7 25.0 %collective-permute-start.1 = (bf16[896,256]{1,0:T(8,128)(2,1)S(1)}, bf16[896,256]{1,0:T(8,128)(2,1)S(1)}, u32[]{:S(2)}, u32[]{:S(2)}) collective-permute-start(bf16[896,256]{1,0:T(8,128)(2,1)S(1)} %slice.3), channel_id=1, source_target_pairs={{0,2},{1,3},{2,0},{3,1},{4,6},{5,7},{6,4},{7,5}} | collective-permute-start | bytes 1376264 | tf_op jit(solution)/shard_map/ppermute | solution.py:397
  5.0 25.3 %collective-permute-start = (bf16[896,384]{1,0:T(8,128)(2,1)}, bf16[896,384]{1,0:T(8,128)(2,1)S(1)}, u32[]{:S(2)}, u32[]{:S(2)}) collective-permute-start(bf16[896,384]{1,0:T(8,128)(2,1)} %wk_h.3), channel_id=1, source_target_pairs={{0,2},{1,3},{2,0},{3,1},{4,6},{5,7},{6,4},{7,5}} | collective-permute-start | bytes 2064392 | tf_op jit(solution)/shard_map/ppermute | solution.py:395
  5.0 25.2 %copy-start = (bf16[16,1536]{1,0:T(8,128)(2,1)S(1)}, bf16[16,1536]{1,0:T(8,128)(2,1)}, u32[]{:S(2)}) copy-start(bf16[16,1536]{1,0:T(8,128)(2,1)} %x_ref.1) | copy-start | bytes 147460
  5.0 25.2 %copy-start.1 = (f32[1536]{0:T(1024)S(1)}, f32[1536]{0:T(1024)}, u32[]{:S(2)}) copy-start(f32[1536]{0:T(1024)} %g2.1) | copy-start | bytes 18436
  5.1 25.2 %copy-start.2 = (f32[1536]{0:T(1024)S(1)}, f32[1536]{0:T(1024)}, u32[]{:S(2)}) copy-start(f32[1536]{0:T(1024)} %b2.1) | copy-start | bytes 18436
  5.1 25.2 %copy-start.3 = (f32[1536]{0:T(1024)S(1)}, f32[1536]{0:T(1024)}, u32[]{:S(2)}) copy-start(f32[1536]{0:T(1024)} %g3.1) | copy-start | bytes 18436
  5.1 25.2 %copy-start.4 = (f32[1536]{0:T(1024)S(1)}, f32[1536]{0:T(1024)}, u32[]{:S(2)}) copy-start(f32[1536]{0:T(1024)} %b3.1) | copy-start | bytes 18436
